TPU v7x, 128 devices: a whole 4x4x4 slice. The times are simulated.
128 devices in a mesh: frames: 16 (over x, y), tile: 8 (over z, core).
Axes of the slice: x: 4, y: 4, z: 4, core: 2. Of those that a mesh axis runs over, the one named last changes fastest.
Arguments:
- latents: bfloat16 [16, 128, 160, 256], P('frames', 'tile'), may hold values from -6 to 6
- conv_first: bfloat16 [3, 3, 256, 256], replicated, may hold values from -0.125 to 0.125
- conv_second: bfloat16 [3, 3, 256, 256], replicated, may hold values from -0.125 to 0.125
- gain_first: float32 [256], replicated, may hold values from 0.25 to 1.75
- gain_second: float32 [256], replicated, may hold values from 0.25 to 1.75
- gain_key: float32 [256], replicated, may hold values from 0.25 to 1.75
- queries: bfloat16 [8192, 2560], P(('frames', 'tile')), may hold values from -140 to 140
- key_weight: bfloat16 [256, 2560], replicated, may hold values from -0.375 to 0.375
- value_weight: bfloat16 [256, 2560], replicated, may hold values from -0.375 to 0.375
- frame_ids: int32 [16, 128], replicated, may hold values from -1 to 15, as said below
- block_ids: int32 [16, 128], replicated, may hold values from -1 to 511, as said below
- counts: int32 [16], replicated, may hold values from 1 to 128, as said below
Outputs:
- refined: bfloat16 [16, 128, 160, 256], P('frames', 'tile')
- attended: bfloat16 [8192, 2560], P(('frames', 'tile'))
Inputs may be any that keep to these rules, and one draw needn't show every extreme that they name: `frame_ids`: entries j < counts[g] name frames; later entries are -1. One owner never lists two blocks that lie in the same frame and the same 16 rows of a tile. `block_ids`: entries j < counts[g] name blocks of a frame; later entries are -1. `counts`: some owner lists 128 blocks in every draw.
All inputs are finite; a program needn't handle non-finite values.
Results may differ from a plain program's by a relative error of at most 0.039.
Values may be sent and summed in bfloat16 or wider, within the bound.
No kernel may reach another device: no remote copies, remote signals or barrier semaphores. Data moves between devices by JAX's collectives and lax.ppermute only.
A program may use at most 64 MiB of HBM per device.

v0:
```python
import jax
import jax.numpy as jnp
from jax import lax
from jax.sharding import PartitionSpec as P

HEADS = 20
HD = 128
QW = 4


EPSILON = 1e-06
NEGATIVE = -1e30


def extended_2(block, sides, width):
    for axis, dim in sides:
        count = lax.axis_size(axis)
        forward = [(i, i + 1) for i in range(count - 1)]
        backward = [(target, source) for source, target in forward]
        low = lax.ppermute(
            lax.slice_in_dim(block, block.shape[dim] - width, None, axis=dim), axis, forward
        )
        high = lax.ppermute(lax.slice_in_dim(block, 0, width, axis=dim), axis, backward)
        block = jnp.concatenate([low, block, high], axis=dim)
    return block


def norm_rows(values, gain):
    wide = values.astype(jnp.float32)
    mean_square = jnp.mean(wide * wide, axis=-1, keepdims=True)
    return wide * lax.rsqrt(mean_square + EPSILON) * gain


def activate(values, gain):
    return jax.nn.silu(norm_rows(values, gain)).astype(jnp.bfloat16)


def convolve(padded, weight, out_rows):
    count_frames = padded.shape[0]
    width = padded.shape[2]
    channels = padded.shape[3]
    widened = jnp.pad(padded, ((0, 0), (0, 0), (1, 1), (0, 0)))
    total = jnp.zeros((count_frames * out_rows * width, channels), jnp.float32)
    for row_step in range(3):
        for col_step in range(3):
            window = widened[
                :, row_step : row_step + out_rows, col_step : col_step + width, :
            ].reshape(-1, channels)
            total = total + jnp.dot(
                window, weight[row_step, col_step], preferred_element_type=jnp.float32
            )
    return total.reshape(count_frames, out_rows, width, channels)


def head_scores(keys_in, weight_pair, query_head, key_mask):
    head_dim = query_head.shape[-1]
    pair = jnp.dot(keys_in, weight_pair, preferred_element_type=jnp.float32)
    key_head = pair[:, :head_dim]
    value_head = pair[:, head_dim:]
    scale = 1.0 / head_dim**0.5
    scores = (
        jnp.einsum(
            "qd,kd->qk", query_head.astype(jnp.float32), key_head, precision=lax.Precision.HIGHEST
        )
        * scale
    )
    scores = jnp.where(key_mask[None, :], scores, NEGATIVE)
    return (scores, value_head)


def weigh_values(weights, value_head):
    rounded = lax.optimization_barrier(weights.astype(jnp.bfloat16))
    return jnp.dot(rounded.astype(jnp.float32), value_head, precision=lax.Precision.HIGHEST)


def attend_whole(keys_in, key_mask, weight_pairs, query_heads):

    def one_head(operands):
        scores, value_head = head_scores(keys_in, operands[0], operands[1], key_mask)
        peak = jnp.max(scores, axis=-1, keepdims=True)
        weights = jnp.exp(scores - peak)
        total = jnp.sum(weights, axis=-1, keepdims=True)
        mixed = weigh_values(weights, value_head)
        return (mixed / total).astype(jnp.bfloat16)

    return lax.map(one_head, (weight_pairs, query_heads))


def local(
    latents,
    conv_first,
    conv_second,
    gain_first,
    gain_second,
    gain_key,
    queries,
    key_weight,
    value_weight,
    frame_ids,
    block_ids,
    counts,
):
    rows = latents.shape[1]
    width = latents.shape[2]
    channels = latents.shape[3]
    tile_count = lax.axis_size("tile")
    frame_count = lax.axis_size("frames")
    tile_index = lax.axis_index("tile")
    frame_index = lax.axis_index("frames")
    extended = extended_2(latents, (("tile", 1),), 2)
    first_act = activate(extended, gain_first)
    middle = (
        extended[:, 1:-1].astype(jnp.float32) + convolve(first_act, conv_first, rows + 2)
    ).astype(jnp.bfloat16)
    global_row = tile_index * rows - 1 + jnp.arange(rows + 2, dtype=jnp.int32)
    inside = (global_row >= 0) & (global_row < rows * tile_count)
    second_act = jnp.where(
        inside[None, :, None, None], activate(middle, gain_second), jnp.zeros((), jnp.bfloat16)
    )
    refined = (
        middle[:, 1:-1].astype(jnp.float32) + convolve(second_act, conv_second, rows)
    ).astype(jnp.bfloat16)
    normed = norm_rows(refined, gain_key).astype(jnp.bfloat16)
    block_tokens = width // QW
    per_tile = rows * QW
    blocks = normed.reshape(per_tile, block_tokens * channels)
    list_len = frame_ids.shape[1]
    slots = jnp.arange(list_len, dtype=jnp.int32)
    live = slots[None, :] < counts[:, None]
    local_id = block_ids - tile_index * per_tile
    hit = live & (frame_ids == frame_index) & (local_id >= 0) & (local_id < per_tile)
    block_range = jnp.arange(per_tile, dtype=jnp.int32)
    selector = jnp.any(
        hit[:, :, None] & (local_id[:, :, None] == block_range[None, None, :]), axis=1
    ).astype(jnp.bfloat16)
    picked = jnp.dot(selector, blocks, preferred_element_type=jnp.float32).astype(jnp.bfloat16)
    picked = picked.reshape(frame_count, block_tokens, channels)
    owner_live = live[frame_index]
    owner_source = frame_ids[frame_index] * tile_count + block_ids[frame_index] // per_tile
    source_range = jnp.arange(frame_count * tile_count, dtype=jnp.int32)
    source_live = jnp.any(
        owner_live[:, None] & (owner_source[:, None] == source_range[None, :]), axis=0
    )
    source_live = source_live.reshape(frame_count, tile_count)
    stacked = jnp.concatenate(
        [key_weight.reshape(channels, HEADS, HD), value_weight.reshape(channels, HEADS, HD)],
        axis=-1,
    )
    weight_pairs = stacked.transpose(1, 0, 2)
    copies = jnp.repeat(picked, tile_count, axis=0)
    arrived = lax.all_to_all(copies, ("frames", "tile"), split_axis=0, concat_axis=0, tiled=True)
    key_mask = jnp.repeat(source_live.reshape(-1), block_tokens)
    query_heads = queries.reshape(queries.shape[0], HEADS, HD).transpose(1, 0, 2)
    heads_out = attend_whole(arrived.reshape(-1, channels), key_mask, weight_pairs, query_heads)
    attended = heads_out.transpose(1, 0, 2).reshape(queries.shape)
    return (refined, attended)


def solution(mesh):
    in_specs = (
        P("frames", "tile", None, None),
        P(),
        P(),
        P(),
        P(),
        P(),
        P(("frames", "tile"), None),
        P(),
        P(),
        P(),
        P(),
        P(),
    )
    out_specs = (P("frames", "tile", None, None), P(("frames", "tile"), None))
    return jax.shard_map(local, mesh=mesh, in_specs=in_specs, out_specs=out_specs, check_vma=False)
```

profile of v0, /device:TPU:1, one launch (start us, length us, event | category | flops | bytes accessed | tf_op | source)
XLA Modules:
  0.0 283.8 jit_solution(1368098239552754970)
XLA Ops:
  1.7 4.9 %collective-permute-start = (bf16[1,2,160,256]{3,2,1,0:T(8,128)(2,1)S(1)}, bf16[1,2,160,256]{3,2,1,0:T(8,128)(2,1)S(1)}, u32[]{:S(2)}, u32[]{:S(2)}) collective-permute-start(bf16[1,2,160,256]{3,2,1,0:T(8,128)(2,1)S(1)} %get-tuple-element.103), channel_id=1, source_target_pairs={{0,1},{1,2},{2,3},{3,4},{4,5},{5,6},{6,7},{8,9},{9,10},{10,11},{11... | collective-permute-start | bytes 491528 | tf_op jit(solution)/shard_map/ppermute | solution.py:20
  15.2 6.0 %pad_slice_fusion = (bf16[1,18,160,256]{3,2,1,0:T(8,128)(2,1)S(1)}, bf16[1,18,160,256]{3,2,1,0:T(8,128)(2,1)S(1)}, bf16[1,18,160,256]{3,2,1,0:T(8,128)(2,1)S(1)}...) fusion(bf16[1,20,160,256]{3,2,1,0:T(8,128)(2,1)S(1)} %fusion.33), kind=kLoop, calls=%fused_computation.66 | loop fusion | bytes 19333120 | tf_op jit(solution)/shard_map/slice | solution.py:46
  28.5 5.6 %pad_slice_fusion.6 = (bf16[1,16,160,256]{3,2,1,0:T(8,128)(2,1)S(1)}, bf16[1,16,160,256]{3,2,1,0:T(8,128)(2,1)S(1)}, bf16[1,16,160,256]{3,2,1,0:T(8,128)(2,1)S(1...) fusion(bf16[1,18,160,256]{3,2,1,0:T(8,128)(2,1)S(1)} %fusion.45), kind=kLoop, calls=%fused_computation.72 | loop fusion | bytes 17203200 | tf_op jit(solution)/shard_map/slice | solution.py:46
  43.8 9.7 %all-to-all-start = ((bf16[128,40,256]{2,1,0:T(8,128)(2,1)}), bf16[128,40,256]{2,1,0:T(8,128)(2,1)S(1)}, u32[]{:S(2)}, u32[]{:S(2)}) async-start(bf16[128,40,256]{2,1,0:T(8,128)(2,1)} %bitcast.153), calls=%async_computation | async-start | bytes 5242880 | tf_op jit(solution)/shard_map/all_to_all | solution.py:151
  63.0 26.5 %all-to-all-done = bf16[128,40,256]{2,1,0:T(8,128)(2,1)S(1)} async-done(((bf16[128,40,256]{2,1,0:T(8,128)(2,1)}), bf16[128,40,256]{2,1,0:T(8,128)(2,1)S(1)}, u32[]{:S(2)}, u32[]{:S(2)}) %all-to-all-start) | async-done | bytes 2621472 | tf_op jit(solution)/shard_map/all_to_all | solution.py:151
  89.5 193.5 %while.11 = (s32[]{:T(128)}, bf16[20,64,128]{2,1,0:T(8,128)(2,1)S(1)}, bf16[20,64,128]{2,1,0:T(8,128)(2,1)S(1)}, bf16[20,256,256]{1,2,0:T(8,128)(2,1)}, bf16[512...) while((s32[]{:T(128)}, bf16[20,64,128]{2,1,0:T(8,128)(2,1)S(1)}, ...), condition=%wide.region_8.9_spmd.clone, body=%wide.region_5.8_spmd.clone.sunk | while | flops 1679704064 | bytes 38197740 | solution.py:86
  99.2 4.1 %convolution_bitcast_fusion.2 = f32[5120,256]{0,1:T(8,128)} fusion(bf16[5120,256]{1,0:T(8,128)(2,1)S(1)} %get-tuple-element.168, bf16[20,256,256]{1,2,0:T(8,128)(2,1)} %get-tuple-element.167, s32[]{:T(128)} %get-tuple-element.157), kind=kOutput, calls=%fused_computation.1.clone.1 | convolution fusion | flops 671088640 | bytes 7995904 | tf_op jit(solution)/shard_map/while/body/eval_jaxpr/dot_general | solution.py:57
  108.9 4.1 %convolution_bitcast_fusion.2 = f32[5120,256]{0,1:T(8,128)} fusion(bf16[5120,256]{1,0:T(8,128)(2,1)S(1)} %get-tuple-element.168, bf16[20,256,256]{1,2,0:T(8,128)(2,1)} %get-tuple-element.167, s32[]{:T(128)} %get-tuple-element.157), kind=kOutput, calls=%fused_computation.1.clone.1 | convolution fusion | flops 671088640 | bytes 7995904 | tf_op jit(solution)/shard_map/while/body/eval_jaxpr/dot_general | solution.py:57
  118.5 4.1 %convolution_bitcast_fusion.2 = f32[5120,256]{0,1:T(8,128)} fusion(bf16[5120,256]{1,0:T(8,128)(2,1)S(1)} %get-tuple-element.168, bf16[20,256,256]{1,2,0:T(8,128)(2,1)} %get-tuple-element.167, s32[]{:T(128)} %get-tuple-element.157), kind=kOutput, calls=%fused_computation.1.clone.1 | convolution fusion | flops 671088640 | bytes 7995904 | tf_op jit(solution)/shard_map/while/body/eval_jaxpr/dot_general | solution.py:57
  128.2 4.1 %convolution_bitcast_fusion.2 = f32[5120,256]{0,1:T(8,128)} fusion(bf16[5120,256]{1,0:T(8,128)(2,1)S(1)} %get-tuple-element.168, bf16[20,256,256]{1,2,0:T(8,128)(2,1)} %get-tuple-element.167, s32[]{:T(128)} %get-tuple-element.157), kind=kOutput, calls=%fused_computation.1.clone.1 | convolution fusion | flops 671088640 | bytes 7995904 | tf_op jit(solution)/shard_map/while/body/eval_jaxpr/dot_general | solution.py:57
  137.9 4.1 %convolution_bitcast_fusion.2 = f32[5120,256]{0,1:T(8,128)} fusion(bf16[5120,256]{1,0:T(8,128)(2,1)S(1)} %get-tuple-element.168, bf16[20,256,256]{1,2,0:T(8,128)(2,1)} %get-tuple-element.167, s32[]{:T(128)} %get-tuple-element.157), kind=kOutput, calls=%fused_computation.1.clone.1 | convolution fusion | flops 671088640 | bytes 7995904 | tf_op jit(solution)/shard_map/while/body/eval_jaxpr/dot_general | solution.py:57
  147.6 4.1 %convolution_bitcast_fusion.2 = f32[5120,256]{0,1:T(8,128)} fusion(bf16[5120,256]{1,0:T(8,128)(2,1)S(1)} %get-tuple-element.168, bf16[20,256,256]{1,2,0:T(8,128)(2,1)} %get-tuple-element.167, s32[]{:T(128)} %get-tuple-element.157), kind=kOutput, calls=%fused_computation.1.clone.1 | convolution fusion | flops 671088640 | bytes 7995904 | tf_op jit(solution)/shard_map/while/body/eval_jaxpr/dot_general | solution.py:57
  157.3 4.1 %convolution_bitcast_fusion.2 = f32[5120,256]{0,1:T(8,128)} fusion(bf16[5120,256]{1,0:T(8,128)(2,1)S(1)} %get-tuple-element.168, bf16[20,256,256]{1,2,0:T(8,128)(2,1)} %get-tuple-element.167, s32[]{:T(128)} %get-tuple-element.157), kind=kOutput, calls=%fused_computation.1.clone.1 | convolution fusion | flops 671088640 | bytes 7995904 | tf_op jit(solution)/shard_map/while/body/eval_jaxpr/dot_general | solution.py:57
  166.9 4.1 %convolution_bitcast_fusion.2 = f32[5120,256]{0,1:T(8,128)} fusion(bf16[5120,256]{1,0:T(8,128)(2,1)S(1)} %get-tuple-element.168, bf16[20,256,256]{1,2,0:T(8,128)(2,1)} %get-tuple-element.167, s32[]{:T(128)} %get-tuple-element.157), kind=kOutput, calls=%fused_computation.1.clone.1 | convolution fusion | flops 671088640 | bytes 7995904 | tf_op jit(solution)/shard_map/while/body/eval_jaxpr/dot_general | solution.py:57
  176.6 4.1 %convolution_bitcast_fusion.2 = f32[5120,256]{0,1:T(8,128)} fusion(bf16[5120,256]{1,0:T(8,128)(2,1)S(1)} %get-tuple-element.168, bf16[20,256,256]{1,2,0:T(8,128)(2,1)} %get-tuple-element.167, s32[]{:T(128)} %get-tuple-element.157), kind=kOutput, calls=%fused_computation.1.clone.1 | convolution fusion | flops 671088640 | bytes 7995904 | tf_op jit(solution)/shard_map/while/body/eval_jaxpr/dot_general | solution.py:57
  186.3 4.1 %convolution_bitcast_fusion.2 = f32[5120,256]{0,1:T(8,128)} fusion(bf16[5120,256]{1,0:T(8,128)(2,1)S(1)} %get-tuple-element.168, bf16[20,256,256]{1,2,0:T(8,128)(2,1)} %get-tuple-element.167, s32[]{:T(128)} %get-tuple-element.157), kind=kOutput, calls=%fused_computation.1.clone.1 | convolution fusion | flops 671088640 | bytes 7995904 | tf_op jit(solution)/shard_map/while/body/eval_jaxpr/dot_general | solution.py:57
  196.0 4.1 %convolution_bitcast_fusion.2 = f32[5120,256]{0,1:T(8,128)} fusion(bf16[5120,256]{1,0:T(8,128)(2,1)S(1)} %get-tuple-element.168, bf16[20,256,256]{1,2,0:T(8,128)(2,1)} %get-tuple-element.167, s32[]{:T(128)} %get-tuple-element.157), kind=kOutput, calls=%fused_computation.1.clone.1 | convolution fusion | flops 671088640 | bytes 7995904 | tf_op jit(solution)/shard_map/while/body/eval_jaxpr/dot_general | solution.py:57
  205.6 4.1 %convolution_bitcast_fusion.2 = f32[5120,256]{0,1:T(8,128)} fusion(bf16[5120,256]{1,0:T(8,128)(2,1)S(1)} %get-tuple-element.168, bf16[20,256,256]{1,2,0:T(8,128)(2,1)} %get-tuple-element.167, s32[]{:T(128)} %get-tuple-element.157), kind=kOutput, calls=%fused_computation.1.clone.1 | convolution fusion | flops 671088640 | bytes 7995904 | tf_op jit(solution)/shard_map/while/body/eval_jaxpr/dot_general | solution.py:57
  215.3 4.1 %convolution_bitcast_fusion.2 = f32[5120,256]{0,1:T(8,128)} fusion(bf16[5120,256]{1,0:T(8,128)(2,1)S(1)} %get-tuple-element.168, bf16[20,256,256]{1,2,0:T(8,128)(2,1)} %get-tuple-element.167, s32[]{:T(128)} %get-tuple-element.157), kind=kOutput, calls=%fused_computation.1.clone.1 | convolution fusion | flops 671088640 | bytes 7995904 | tf_op jit(solution)/shard_map/while/body/eval_jaxpr/dot_general | solution.py:57
  225.0 4.1 %convolution_bitcast_fusion.2 = f32[5120,256]{0,1:T(8,128)} fusion(bf16[5120,256]{1,0:T(8,128)(2,1)S(1)} %get-tuple-element.168, bf16[20,256,256]{1,2,0:T(8,128)(2,1)} %get-tuple-element.167, s32[]{:T(128)} %get-tuple-element.157), kind=kOutput, calls=%fused_computation.1.clone.1 | convolution fusion | flops 671088640 | bytes 7995904 | tf_op jit(solution)/shard_map/while/body/eval_jaxpr/dot_general | solution.py:57
  234.7 4.1 %convolution_bitcast_fusion.2 = f32[5120,256]{0,1:T(8,128)} fusion(bf16[5120,256]{1,0:T(8,128)(2,1)S(1)} %get-tuple-element.168, bf16[20,256,256]{1,2,0:T(8,128)(2,1)} %get-tuple-element.167, s32[]{:T(128)} %get-tuple-element.157), kind=kOutput, calls=%fused_computation.1.clone.1 | convolution fusion | flops 671088640 | bytes 7995904 | tf_op jit(solution)/shard_map/while/body/eval_jaxpr/dot_general | solution.py:57
  244.3 4.1 %convolution_bitcast_fusion.2 = f32[5120,256]{0,1:T(8,128)} fusion(bf16[5120,256]{1,0:T(8,128)(2,1)S(1)} %get-tuple-element.168, bf16[20,256,256]{1,2,0:T(8,128)(2,1)} %get-tuple-element.167, s32[]{:T(128)} %get-tuple-element.157), kind=kOutput, calls=%fused_computation.1.clone.1 | convolution fusion | flops 671088640 | bytes 7995904 | tf_op jit(solution)/shard_map/while/body/eval_jaxpr/dot_general | solution.py:57
  254.0 4.1 %convolution_bitcast_fusion.2 = f32[5120,256]{0,1:T(8,128)} fusion(bf16[5120,256]{1,0:T(8,128)(2,1)S(1)} %get-tuple-element.168, bf16[20,256,256]{1,2,0:T(8,128)(2,1)} %get-tuple-element.167, s32[]{:T(128)} %get-tuple-element.157), kind=kOutput, calls=%fused_computation.1.clone.1 | convolution fusion | flops 671088640 | bytes 7995904 | tf_op jit(solution)/shard_map/while/body/eval_jaxpr/dot_general | solution.py:57
  273.4 4.1 %convolution_bitcast_fusion.2 = f32[5120,256]{0,1:T(8,128)} fusion(bf16[5120,256]{1,0:T(8,128)(2,1)S(1)} %get-tuple-element.168, bf16[20,256,256]{1,2,0:T(8,128)(2,1)} %get-tuple-element.167, s32[]{:T(128)} %get-tuple-element.157), kind=kOutput, calls=%fused_computation.1.clone.1 | convolution fusion | flops 671088640 | bytes 7995904 | tf_op jit(solution)/shard_map/while/body/eval_jaxpr/dot_general | solution.py:57
  (209 shorter events, 155.7 us)
Async XLA Ops:
  1.7 8.0 %collective-permute-start = (bf16[1,2,160,256]{3,2,1,0:T(8,128)(2,1)S(1)}, bf16[1,2,160,256]{3,2,1,0:T(8,128)(2,1)S(1)}, u32[]{:S(2)}, u32[]{:S(2)}) collective-permute-start(bf16[1,2,160,256]{3,2,1,0:T(8,128)(2,1)S(1)} %get-tuple-element.103), channel_id=1, source_target_pairs={{0,1},{1,2},{2,3},{3,4},{4,5},{5,6},{6,7},{8,9},{9,10},{10,11},{11... | collective-permute-start | bytes 491528 | tf_op jit(solution)/shard_map/ppermute | solution.py:20
  6.6 6.6 %collective-permute-start.1 = (bf16[1,2,160,256]{3,2,1,0:T(8,128)(2,1)S(1)}, bf16[1,2,160,256]{3,2,1,0:T(8,128)(2,1)S(1)}, u32[]{:S(2)}, u32[]{:S(2)}) collective-permute-start(bf16[1,2,160,256]{3,2,1,0:T(8,128)(2,1)S(1)} %get-tuple-element.102), channel_id=1, source_target_pairs={{1,0},{2,1},{3,2},{4,3},{5,4},{6,5},{7,6},{9,8},{10,9},{11,10},{12... | collective-permute-start | bytes 491528 | tf_op jit(solution)/shard_map/ppermute | solution.py:23
  15.2 6.0 %copy-start.2 = (bf16[3,3,256,256]{3,2,1,0:T(8,128)(2,1)S(1)}, bf16[3,3,256,256]{3,2,1,0:T(8,128)(2,1)}, u32[]{:S(2)}) copy-start(bf16[3,3,256,256]{3,2,1,0:T(8,128)(2,1)} %param.15) | copy-start | bytes 3538948
  28.5 5.6 %copy-start.3 = (bf16[3,3,256,256]{3,2,1,0:T(8,128)(2,1)S(1)}, bf16[3,3,256,256]{3,2,1,0:T(8,128)(2,1)}, u32[]{:S(2)}) copy-start(bf16[3,3,256,256]{3,2,1,0:T(8,128)(2,1)} %param.16) | copy-start | bytes 3538948
  43.8 45.7 %all-to-all-start = ((bf16[128,40,256]{2,1,0:T(8,128)(2,1)}), bf16[128,40,256]{2,1,0:T(8,128)(2,1)S(1)}, u32[]{:S(2)}, u32[]{:S(2)}) async-start(bf16[128,40,256]{2,1,0:T(8,128)(2,1)} %bitcast.153), calls=%async_computation | async-start | bytes 5242880 | tf_op jit(solution)/shard_map/all_to_all | solution.py:151
  59.5 30.0 %copy-start.5 = (bf16[20,64,128]{2,1,0:T(8,128)(2,1)S(1)}, bf16[20,64,128]{2,1,0:T(8,128)(2,1)}, u32[]{:S(2)}) copy-start(bf16[20,64,128]{2,1,0:T(8,128)(2,1)} %custom-call.1) | copy-start | bytes 983044
  93.8 3.7 %copy-start = (f32[5120,256]{0,1:T(8,128)S(1)}, f32[5120,256]{0,1:T(8,128)}, u32[]{:S(2)}) copy-start(f32[5120,256]{0,1:T(8,128)} %convolution_bitcast_fusion.2) | copy-start | bytes 15728644 | tf_op jit(solution)/shard_map/while
  103.5 3.7 %copy-start = (f32[5120,256]{0,1:T(8,128)S(1)}, f32[5120,256]{0,1:T(8,128)}, u32[]{:S(2)}) copy-start(f32[5120,256]{0,1:T(8,128)} %convolution_bitcast_fusion.2) | copy-start | bytes 15728644 | tf_op jit(solution)/shard_map/while
  113.2 3.7 %copy-start = (f32[5120,256]{0,1:T(8,128)S(1)}, f32[5120,256]{0,1:T(8,128)}, u32[]{:S(2)}) copy-start(f32[5120,256]{0,1:T(8,128)} %convolution_bitcast_fusion.2) | copy-start | bytes 15728644 | tf_op jit(solution)/shard_map/while
  122.8 3.7 %copy-start = (f32[5120,256]{0,1:T(8,128)S(1)}, f32[5120,256]{0,1:T(8,128)}, u32[]{:S(2)}) copy-start(f32[5120,256]{0,1:T(8,128)} %convolution_bitcast_fusion.2) | copy-start | bytes 15728644 | tf_op jit(solution)/shard_map/while
  132.5 3.7 %copy-start = (f32[5120,256]{0,1:T(8,128)S(1)}, f32[5120,256]{0,1:T(8,128)}, u32[]{:S(2)}) copy-start(f32[5120,256]{0,1:T(8,128)} %convolution_bitcast_fusion.2) | copy-start | bytes 15728644 | tf_op jit(solution)/shard_map/while
  142.2 3.7 %copy-start = (f32[5120,256]{0,1:T(8,128)S(1)}, f32[5120,256]{0,1:T(8,128)}, u32[]{:S(2)}) copy-start(f32[5120,256]{0,1:T(8,128)} %convolution_bitcast_fusion.2) | copy-start | bytes 15728644 | tf_op jit(solution)/shard_map/while
  151.9 3.7 %copy-start = (f32[5120,256]{0,1:T(8,128)S(1)}, f32[5120,256]{0,1:T(8,128)}, u32[]{:S(2)}) copy-start(f32[5120,256]{0,1:T(8,128)} %convolution_bitcast_fusion.2) | copy-start | bytes 15728644 | tf_op jit(solution)/shard_map/while
  161.5 3.7 %copy-start = (f32[5120,256]{0,1:T(8,128)S(1)}, f32[5120,256]{0,1:T(8,128)}, u32[]{:S(2)}) copy-start(f32[5120,256]{0,1:T(8,128)} %convolution_bitcast_fusion.2) | copy-start | bytes 15728644 | tf_op jit(solution)/shard_map/while
  171.2 3.7 %copy-start = (f32[5120,256]{0,1:T(8,128)S(1)}, f32[5120,256]{0,1:T(8,128)}, u32[]{:S(2)}) copy-start(f32[5120,256]{0,1:T(8,128)} %convolution_bitcast_fusion.2) | copy-start | bytes 15728644 | tf_op jit(solution)/shard_map/while
  180.9 3.7 %copy-start = (f32[5120,256]{0,1:T(8,128)S(1)}, f32[5120,256]{0,1:T(8,128)}, u32[]{:S(2)}) copy-start(f32[5120,256]{0,1:T(8,128)} %convolution_bitcast_fusion.2) | copy-start | bytes 15728644 | tf_op jit(solution)/shard_map/while
  190.6 3.7 %copy-start = (f32[5120,256]{0,1:T(8,128)S(1)}, f32[5120,256]{0,1:T(8,128)}, u32[]{:S(2)}) copy-start(f32[5120,256]{0,1:T(8,128)} %convolution_bitcast_fusion.2) | copy-start | bytes 15728644 | tf_op jit(solution)/shard_map/while
  200.2 3.7 %copy-start = (f32[5120,256]{0,1:T(8,128)S(1)}, f32[5120,256]{0,1:T(8,128)}, u32[]{:S(2)}) copy-start(f32[5120,256]{0,1:T(8,128)} %convolution_bitcast_fusion.2) | copy-start | bytes 15728644 | tf_op jit(solution)/shard_map/while
  209.9 3.7 %copy-start = (f32[5120,256]{0,1:T(8,128)S(1)}, f32[5120,256]{0,1:T(8,128)}, u32[]{:S(2)}) copy-start(f32[5120,256]{0,1:T(8,128)} %convolution_bitcast_fusion.2) | copy-start | bytes 15728644 | tf_op jit(solution)/shard_map/while
  219.6 3.7 %copy-start = (f32[5120,256]{0,1:T(8,128)S(1)}, f32[5120,256]{0,1:T(8,128)}, u32[]{:S(2)}) copy-start(f32[5120,256]{0,1:T(8,128)} %convolution_bitcast_fusion.2) | copy-start | bytes 15728644 | tf_op jit(solution)/shard_map/while
  229.3 3.7 %copy-start = (f32[5120,256]{0,1:T(8,128)S(1)}, f32[5120,256]{0,1:T(8,128)}, u32[]{:S(2)}) copy-start(f32[5120,256]{0,1:T(8,128)} %convolution_bitcast_fusion.2) | copy-start | bytes 15728644 | tf_op jit(solution)/shard_map/while
  238.9 3.7 %copy-start = (f32[5120,256]{0,1:T(8,128)S(1)}, f32[5120,256]{0,1:T(8,128)}, u32[]{:S(2)}) copy-start(f32[5120,256]{0,1:T(8,128)} %convolution_bitcast_fusion.2) | copy-start | bytes 15728644 | tf_op jit(solution)/shard_map/while
  258.3 3.7 %copy-start = (f32[5120,256]{0,1:T(8,128)S(1)}, f32[5120,256]{0,1:T(8,128)}, u32[]{:S(2)}) copy-start(f32[5120,256]{0,1:T(8,128)} %convolution_bitcast_fusion.2) | copy-start | bytes 15728644 | tf_op jit(solution)/shard_map/while
  277.7 3.7 %copy-start = (f32[5120,256]{0,1:T(8,128)S(1)}, f32[5120,256]{0,1:T(8,128)}, u32[]{:S(2)}) copy-start(f32[5120,256]{0,1:T(8,128)} %convolution_bitcast_fusion.2) | copy-start | bytes 15728644 | tf_op jit(solution)/shard_map/while
  (7 other events, 16.3 us)
where the time goes:
time: 285 us; the launch traced here: 284 us
  matrix products  191 us (67%)
  waiting for transfers between devices  28.6 us (10%)
  local copies, waits for them, and re-layouts  27.3 us (10%)
  other arithmetic  18.1 us (6%)
  starting transfers between devices  16.5 us (6%)
    dot_general x20, matrix products, head_scores(): pair = jnp.dot(keys_in, weight_pair, preferred_element_type=jnp.float32)  81.8 us
    dot_general x20, matrix products, head_scores(): jnp.einsum('qd,kd->qk', query_head.astype(jnp.float32), key_head, precisi...  66.4 us
    dot_general x20, matrix products, weigh_values(): jnp.dot(rounded.astype(jnp.float32), value_head, precision=lax.Precision....  33 us
    all_to_all x1, waiting for transfers between devices, local(): lax.all_to_all(copies, ('frames', 'tile'), split_axis=0, concat_axis=0, t...  26.5 us
    slice x2, local copies, waits for them, and re-layouts, convolve(): widened[:, row_step:row_step + out_rows, col_step:col_step + width, :]  11.6 us
    dot_general x18, matrix products, convolve(): jnp.dot(window, weight[row_step, col_step], preferred_element_type=jnp.fl...  10 us
    all_to_all x1, starting transfers between devices, local(): lax.all_to_all(copies, ('frames', 'tile'), split_axis=0, concat_axis=0, t...  9.65 us
    reduce_sum x20, other arithmetic, one_head(): total = jnp.sum(weights, axis=-1, keepdims=True)  7.66 us
  transfers between devices with their start and end apart: 3, of which 2 were waited for; matrix products, arithmetic and copies ran while one was open for 4% of the time, Pallas kernels for 0%

commit v1 on v0

v1 whole, which is shorter than its diff:
```python
import functools

import jax
import jax.numpy as jnp
from jax import lax
from jax.experimental import pallas as pl
from jax.experimental.pallas import tpu as pltpu
from jax.sharding import PartitionSpec as P

C = 256
HEADS = 20
HD = 128
QW = 4
BT = 40
W = 160
ROWS = 16
Q_DEV = 64
FRAMES = 16
TILES = 8
QROWS = HEADS * Q_DEV
EPSILON = 1e-06
NEGATIVE = -1e30
LOG2E = 1.4426950408889634
VMEM = pl.BlockSpec(memory_space=pltpu.VMEM)
SMEM = pl.BlockSpec(memory_space=pltpu.SMEM)


def normalized(wide, gain):
    mean_square = jnp.mean(wide * wide, axis=-1, keepdims=True)
    return wide * lax.rsqrt(mean_square + EPSILON) * gain


def store_windows(act, dst_ref, row):
    column = lax.broadcasted_iota(jnp.int32, act.shape, 0)
    left = jnp.where(column == 0, 0.0, pltpu.roll(act, 1, 0))
    right = jnp.where(column == W - 1, 0.0, pltpu.roll(act, W - 1, 0))
    dst_ref[row, :, 0:C] = left.astype(jnp.bfloat16)
    dst_ref[row, :, C : 2 * C] = act.astype(jnp.bfloat16)
    dst_ref[row, :, 2 * C : 3 * C] = right.astype(jnp.bfloat16)


def silu_norm(wide, half_gain):
    half = normalized(wide, half_gain)
    return half + half * jnp.tanh(half)


def windows_dot(src_ref, weight_ref, row, count):
    total = None
    for step in range(3):
        window = src_ref[row + step : row + step + count].reshape(count * W, 3 * C)
        part = jnp.dot(window, weight_ref[step], preferred_element_type=jnp.float32)
        total = part if total is None else total + part
    return total


def conv_kernel(
    pick_ref, edge_ref, x_ref, low_ref, high_ref, w1_ref, w2_ref, g1_ref, g2_ref, gk_ref,
    refined_ref, picked_ref, first_ref, middle_ref, second_ref, wide_ref,
):
    g1 = g1_ref[...] * 0.5
    g2 = g2_ref[...] * 0.5

    def first_row(source, row):
        store_windows(silu_norm(source.astype(jnp.float32), g1), first_ref, row)

    for k in range(2):
        first_row(low_ref[k], k)
        first_row(high_ref[k], ROWS + 2 + k)
    for k in range(ROWS):
        first_row(x_ref[k], k + 2)

    group = 6
    for start in range(0, ROWS + 2, group):
        total = windows_dot(first_ref, w1_ref, start, group)
        for k in range(group):
            row = start + k
            if row == 0:
                base = low_ref[1]
            elif row == ROWS + 1:
                base = high_ref[0]
            else:
                base = x_ref[row - 1]
            middle = (base.astype(jnp.float32) + total[k * W : (k + 1) * W]).astype(jnp.bfloat16)
            middle_ref[row] = middle
            act = silu_norm(middle.astype(jnp.float32), g2)
            if row == 0:
                act = act * edge_ref[0]
            if row == ROWS + 1:
                act = act * edge_ref[1]
            store_windows(act, second_ref, row)

    group = 8
    for start in range(0, ROWS, group):
        total = windows_dot(second_ref, w2_ref, start, group)
        for k in range(group):
            row = start + k
            out = middle_ref[row + 1].astype(jnp.float32) + total[k * W : (k + 1) * W]
            out = out.astype(jnp.bfloat16)
            refined_ref[row] = out
            wide_ref[row * W : (row + 1) * W] = out.astype(jnp.float32)

    gk = gk_ref[...]
    for g in range(FRAMES):
        at = pl.multiple_of(pick_ref[g] * BT, 8)
        block = normalized(wide_ref[pl.ds(at, BT)], gk)
        picked_ref[g] = block.astype(jnp.bfloat16)


def conv_call(pick, edge, latents, low, high, w1, w2, g1, g2, gk):
    return pl.pallas_call(
        conv_kernel,
        name="convs",
        out_shape=(
            jax.ShapeDtypeStruct((ROWS, W, C), jnp.bfloat16),
            jax.ShapeDtypeStruct((FRAMES, BT, C), jnp.bfloat16),
        ),
        in_specs=[SMEM, SMEM] + [VMEM] * 8,
        out_specs=(VMEM, VMEM),
        scratch_shapes=[
            pltpu.VMEM((ROWS + 4, W, 3 * C), jnp.bfloat16),
            pltpu.VMEM((ROWS + 2, W, C), jnp.bfloat16),
            pltpu.VMEM((ROWS + 2, W, 3 * C), jnp.bfloat16),
            pltpu.VMEM((ROWS * W, C), jnp.float32),
        ],
        compiler_params=pltpu.CompilerParams(vmem_limit_bytes=40 * 1024 * 1024),
        cost_estimate=pl.CostEstimate(
            flops=2 * 9 * C * C * W * (2 * ROWS + 2), bytes_accessed=6 << 20, transcendentals=0
        ),
    )(pick, edge, latents, low, high, w1, w2, g1, g2, gk)


def query_kernel(q_ref, wk_ref, high_ref, low_ref):
    scale = LOG2E / HD**0.5
    for h in range(HEADS):
        cols = slice(h * HD, (h + 1) * HD)
        turned = lax.dot_general(
            q_ref[:, cols], wk_ref[:, cols], (((1,), (1,)), ((), ())),
            preferred_element_type=jnp.float32,
        ) * scale
        high = turned.astype(jnp.bfloat16)
        high_ref[h * Q_DEV : (h + 1) * Q_DEV] = high
        low_ref[h * Q_DEV : (h + 1) * Q_DEV] = (turned - high.astype(jnp.float32)).astype(
            jnp.bfloat16
        )


def query_call(queries, key_weight):
    shape = jax.ShapeDtypeStruct((QROWS, C), jnp.bfloat16)
    return pl.pallas_call(
        query_kernel,
        name="turn_queries",
        out_shape=(shape, shape),
        in_specs=[VMEM, VMEM],
        out_specs=(VMEM, VMEM),
        compiler_params=pltpu.CompilerParams(vmem_limit_bytes=16 * 1024 * 1024),
        cost_estimate=pl.CostEstimate(
            flops=2 * QROWS * HD * C, bytes_accessed=3 << 20, transcendentals=0
        ),
    )(queries, key_weight)


BLOCK = 320
SLAB = 32


def attend_kernel(first, last, parts, *refs):
    refs = list(refs)
    qh_ref, ql_ref = refs[:2]
    x_refs = refs[2 : 2 + parts]
    bias_ref = refs[2 + parts]
    refs = refs[3 + parts :]
    if not first:
        m_in, l_in, acc_in = refs[:3]
        refs = refs[3:]
    if last:
        wv_ref, out_ref = refs[:2]
        refs = refs[2:]
    else:
        m_out, l_out, acc_out = refs[:3]
        refs = refs[3:]
    x_ref, s_ref, p_ref = refs
    tokens = x_ref.shape[0]
    at = 0
    for part in x_refs:
        size = part.shape[0] * part.shape[1]
        x_ref[at : at + size] = part[...].reshape(size, C)
        at += size
    bias = bias_ref[...]

    def scores(block, slot):
        rows = slice(block * BLOCK, (block + 1) * BLOCK)
        dims = (((1,), (1,)), ((), ()))
        s_ref[slot] = lax.dot_general(
            qh_ref[rows], x_ref[...], dims, preferred_element_type=jnp.float32
        ) + lax.dot_general(ql_ref[rows], x_ref[...], dims, preferred_element_type=jnp.float32)

    blocks = QROWS // BLOCK
    scores(0, 0)
    for block in range(blocks):
        slot = block % 2
        if block + 1 < blocks:
            scores(block + 1, 1 - slot)
        alphas = []
        sums = []
        for slab in range(BLOCK // SLAB):
            own = slice(slab * SLAB, (slab + 1) * SLAB)
            rows = slice(block * BLOCK + slab * SLAB, block * BLOCK + (slab + 1) * SLAB)
            s = s_ref[slot, own] + bias
            peak = jnp.max(s, axis=-1, keepdims=True)
            if not first:
                old = m_in[rows, 0:1]
                peak = jnp.maximum(peak, old)
                alphas.append(jnp.exp2(old - peak))
            p = jnp.exp2(s - peak)
            total = jnp.sum(p, axis=-1, keepdims=True)
            if not first:
                total = total + alphas[-1] * l_in[rows, 0:1]
            p_ref[slot, own] = p.astype(jnp.bfloat16)
            if last:
                sums.append(total)
            else:
                m_out[rows] = jnp.broadcast_to(peak, (SLAB, 128))
                l_out[rows] = jnp.broadcast_to(total, (SLAB, 128))
        rows = slice(block * BLOCK, (block + 1) * BLOCK)
        mixed = jnp.dot(p_ref[slot], x_ref[...], preferred_element_type=jnp.float32)
        if not first:
            mixed = mixed + jnp.concatenate(alphas, 0) * acc_in[rows]
        if not last:
            acc_out[rows] = mixed
        else:
            mixed = mixed / jnp.concatenate(sums, 0)
            high = mixed.astype(jnp.bfloat16)
            low = (mixed - high.astype(jnp.float32)).astype(jnp.bfloat16)
            for k in range(BLOCK // Q_DEV):
                h = block * (BLOCK // Q_DEV) + k
                cols = slice(h * HD, (h + 1) * HD)
                own = slice(k * Q_DEV, (k + 1) * Q_DEV)
                both = jnp.concatenate([high[own], low[own]], 0)
                value = jnp.dot(both, wv_ref[:, cols], preferred_element_type=jnp.float32)
                out_ref[:, cols] = (value[:Q_DEV] + value[Q_DEV:]).astype(jnp.bfloat16)


def attend_call(qh, ql, parts, bias, state=None, value_weight=None):
    first = state is None
    last = value_weight is not None
    tokens = sum(part.shape[0] * part.shape[1] for part in parts)
    operands = [qh, ql, *parts, bias]
    aliases = {}
    if not first:
        if not last:
            aliases = {len(operands) + k: k for k in range(3)}
        operands += list(state)
    if last:
        operands.append(value_weight)
        out_shape = jax.ShapeDtypeStruct((Q_DEV, HEADS * HD), jnp.bfloat16)
        out_specs = VMEM
    else:
        stat = jax.ShapeDtypeStruct((QROWS, 128), jnp.float32)
        out_shape = (stat, stat, jax.ShapeDtypeStruct((QROWS, C), jnp.float32))
        out_specs = (VMEM, VMEM, VMEM)
    return pl.pallas_call(
        functools.partial(attend_kernel, first, last, len(parts)),
        name="attend",
        out_shape=out_shape,
        in_specs=[VMEM] * len(operands),
        out_specs=out_specs,
        input_output_aliases=aliases,
        scratch_shapes=[
            pltpu.VMEM((tokens, C), jnp.bfloat16),
            pltpu.VMEM((2, BLOCK, tokens), jnp.float32),
            pltpu.VMEM((2, BLOCK, tokens), jnp.bfloat16),
        ],
        compiler_params=pltpu.CompilerParams(vmem_limit_bytes=40 * 1024 * 1024),
        cost_estimate=pl.CostEstimate(
            flops=6 * QROWS * C * tokens, bytes_accessed=6 << 20, transcendentals=QROWS * tokens
        ),
    )(*operands)


def core_swap(x):
    return lax.ppermute(x, "tile", [(t, t ^ 1) for t in range(TILES)])


def turn(x, by):
    pairs = [(t, 2 * ((t // 2 + by) % 4) + t % 2) for t in range(TILES)]
    return lax.ppermute(x, "tile", pairs)


def local(
    latents, conv_first, conv_second, gain_first, gain_second, gain_key,
    queries, key_weight, value_weight, frame_ids, block_ids, counts,
):
    tile = lax.axis_index("tile")
    frame = lax.axis_index("frames")
    forward = [(i, i + 1) for i in range(TILES - 1)]
    backward = [(i + 1, i) for i in range(TILES - 1)]
    own = latents[0]
    low = lax.ppermute(own[ROWS - 2 :], "tile", forward)
    high = lax.ppermute(own[:2], "tile", backward)

    slots = jnp.arange(frame_ids.shape[1], dtype=jnp.int32)
    live = slots[None, :] < counts[:, None]
    per_tile = ROWS * QW
    local_id = block_ids - tile * per_tile
    hit = live & (frame_ids == frame) & (local_id >= 0) & (local_id < per_tile)
    pick = jnp.sum(jnp.where(hit, local_id, 0), axis=1, dtype=jnp.int32)
    edge = jnp.stack([tile > 0, tile < TILES - 1]).astype(jnp.float32)

    depth, core = tile // 2, tile % 2
    order = []
    for by in (0, -1, 1):
        z = (depth + by) % 4
        order += [2 * z + core, 2 * z + 1 - core]
    order = [order[0], order[1], order[2], order[4], order[3], order[5]]
    z = (depth + 2) % 4
    order = jnp.stack(order + [2 * z + core, 2 * z + 1 - core])
    own_live = live[frame]
    own_frames = frame_ids[frame]
    own_tiles = block_ids[frame] // per_tile
    there = (
        own_live[None, None, :]
        & (own_frames[None, None, :] == jnp.arange(FRAMES, dtype=jnp.int32)[None, :, None])
        & (own_tiles[None, None, :] == order[:, None, None])
    ).any(-1)
    bias = jnp.where(there, 0.0, NEGATIVE).astype(jnp.float32)
    bias = jnp.repeat(bias, BT, axis=1).reshape(4, 1, 2 * FRAMES * BT)

    qh, ql = query_call(queries, key_weight)
    refined, picked = conv_call(
        pick, edge, own, low, high,
        conv_first.reshape(3, 3 * C, C), conv_second.reshape(3, 3 * C, C),
        gain_first[None], gain_second[None], gain_key[None],
    )
    mine = lax.all_to_all(picked, "frames", split_axis=0, concat_axis=0, tiled=True)
    partner = core_swap(mine)
    below = turn(mine, 1)
    above = turn(mine, -1)
    half = FRAMES // 2
    far_low = turn(below[:half], 1)
    far_high = turn(above[half:], -1)
    below_swap = core_swap(below)
    above_swap = core_swap(above)
    far_low_swap = core_swap(far_low)
    far_high_swap = core_swap(far_high)
    state = attend_call(qh, ql, (mine, partner), bias[0])
    state = attend_call(qh, ql, (below, above), bias[1], state)
    state = attend_call(qh, ql, (below_swap, above_swap), bias[2], state)
    attended = attend_call(
        qh, ql, (far_low, far_high, far_low_swap, far_high_swap), bias[3], state, value_weight
    )
    return (refined[None], attended)


def solution(mesh):
    in_specs = (
        P("frames", "tile", None, None),
        P(), P(), P(), P(), P(),
        P(("frames", "tile"), None),
        P(), P(), P(), P(), P(),
    )
    out_specs = (P("frames", "tile", None, None), P(("frames", "tile"), None))
    return jax.shard_map(local, mesh=mesh, in_specs=in_specs, out_specs=out_specs, check_vma=False)
```

time: 285 us -> 77.4 us (0.27)
  matrix products: 191 us -> 0 us
  Pallas kernels: 0 us -> 26.9 us
  local copies, waits for them, and re-layouts: 27.3 us -> 8.4 us
  other arithmetic: 18.1 us -> 2.72 us
  waiting for transfers between devices: 28.6 us -> 15.6 us
  starting transfers between devices: 16.5 us -> 22.4 us
    dot_general x79 -> x0, matrix products: 191 us -> none  [the longest x20 81.8 us: head_scores(): pair = jnp.dot(keys_in, weight_pair, preferred_element_type=jnp.float32)]
    pallas_call x0 -> x6, Pallas kernels: none -> 26.9 us  [the longest x4 16.6 us: attend_call(): pl.pallas_call(functools.partial(attend_kernel, first, last, len(parts)),...]
    all_to_all x1, waiting for transfers between devices: 26.5 us -> 7.37 us  [local(): lax.all_to_all(picked, 'frames', split_axis=0, concat_axis=0, tiled=True)]
    slice x3 -> x4, local copies, waits for them, and re-layouts: 12.6 us -> 1.05 us  [the longest x1 1.02 us: local(): high = lax.ppermute(own[:2], 'tile', backward)]
    reduce_sum x23 -> x1, other arithmetic: 9.8 us -> 0.9 us  [local(): pick = jnp.sum(jnp.where(hit, local_id, 0), axis=1, dtype=jnp.int32)]
    ppermute x2 -> x11, starting transfers between devices: 6.84 us -> 15.7 us  [the longest x4 6.75 us: turn(): return lax.ppermute(x, 'tile', pairs)]
    ppermute x2 -> x11, waiting for transfers between devices: 2.07 us -> 8.27 us  [the longest x4 6.8 us: turn(): return lax.ppermute(x, 'tile', pairs)]
    broadcast_in_dim x41 -> x4, local copies, waits for them, and re-layouts: 5.49 us -> 0.28 us  [local(): bias = jnp.repeat(bias, BT, axis=1).reshape(4, 1, 2 * FRAMES * BT)]
  transfers between devices with their start and end apart: 3 -> 12, of which waited for: 2 -> 3; matrix products, arithmetic and copies ran while one was open for 4% -> 5% of each run, Pallas kernels for 0% -> 16%
where the time goes in v1:
time: 77.4 us; the launch traced here: 76.9 us
  Pallas kernels  26.9 us (35%)
  starting transfers between devices  22.4 us (29%)
  waiting for transfers between devices  15.6 us (20%)
  local copies, waits for them, and re-layouts  8.4 us (11%)
  other arithmetic  2.72 us (4%)
  between operations  0.83 us (1%)
    pallas_call x4, Pallas kernels, attend_call(): pl.pallas_call(functools.partial(attend_kernel, first, last, len(parts)),...  16.6 us
    pallas_call x1, Pallas kernels, conv_call(): pl.pallas_call(conv_kernel, name='convs', out_shape=(jax.ShapeDtypeStruct...  9.68 us
    all_to_all x1, waiting for transfers between devices, local(): lax.all_to_all(picked, 'frames', split_axis=0, concat_axis=0, tiled=True)  7.37 us
    ppermute x4, waiting for transfers between devices, turn(): return lax.ppermute(x, 'tile', pairs)  6.8 us
    all_to_all x1, starting transfers between devices, local(): lax.all_to_all(picked, 'frames', split_axis=0, concat_axis=0, tiled=True)  6.75 us
    ppermute x4, starting transfers between devices, turn(): return lax.ppermute(x, 'tile', pairs)  6.75 us
    unnamed x18, local copies, waits for them, and re-layouts  5.9 us
    ppermute x1, starting transfers between devices, local(): low = lax.ppermute(own[ROWS - 2:], 'tile', forward)  4.92 us
  transfers between devices with their start and end apart: 12, of which 3 were waited for; matrix products, arithmetic and copies ran while one was open for 5% of the time, Pallas kernels for 16%

profile of v1, /device:TPU:1, one launch (start us, length us, event | category | flops | bytes accessed | tf_op | source)
XLA Modules:
  0.0 76.9 jit_solution(5261406920322889298)
XLA Ops:
  0.6 1.0 %slice_bitcast_fusion = (bf16[2,160,256]{2,1,0:T(8,128)(2,1)S(1)}, bf16[2,160,256]{2,1,0:T(8,128)(2,1)S(1)}) fusion(bf16[1,16,160,256]{3,2,1,0:T(8,128)(2,1)} %param.12), kind=kLoop, calls=%fused_computation | loop fusion | bytes 655360 | tf_op jit(solution)/shard_map/slice | solution.py:299
  1.7 4.9 %collective-permute-start = (bf16[2,160,256]{2,1,0:T(8,128)(2,1)S(1)}, bf16[2,160,256]{2,1,0:T(8,128)(2,1)S(1)}, u32[]{:S(2)}, u32[]{:S(2)}) collective-permute-start(bf16[2,160,256]{2,1,0:T(8,128)(2,1)S(1)} %get-tuple-element.29), channel_id=1, source_target_pairs={{0,1},{1,2},{2,3},{3,4},{4,5},{5,6},{6,7},{8,9},{9,10},{10,11},{11... | collective-permute-start | bytes 491528 | tf_op jit(solution)/shard_map/ppermute | solution.py:298
  6.6 1.9 %collective-permute-start.1 = (bf16[2,160,256]{2,1,0:T(8,128)(2,1)S(1)}, bf16[2,160,256]{2,1,0:T(8,128)(2,1)S(1)}, u32[]{:S(2)}, u32[]{:S(2)}) collective-permute-start(bf16[2,160,256]{2,1,0:T(8,128)(2,1)S(1)} %get-tuple-element.28), channel_id=1, source_target_pairs={{1,0},{2,1},{3,2},{4,3},{5,4},{6,5},{7,6},{9,8},{10,9},{11,10},{12... | collective-permute-start | bytes 491528 | tf_op jit(solution)/shard_map/ppermute | solution.py:299
  8.5 0.7 iota_compare_fusion.1
  9.2 0.7 and_select_fusion
  10.0 0.7 fusion.1
  10.9 0.9 %select_reduce_fusion.pick_ref = s32[16]{0:T(128)S(1)} fusion(s32[16,128]{1,0:T(8,128)} %param.22, s32[16,128]{1,0:T(8,128)} %param.21, s32[]{:T(128)S(6)} %mul.19, s32[]{:T(128)S(6)} %axis_index.23, s32[16]{0:T(128)} %param.23), kind=kLoop, calls=%fused_computation.4 | loop fusion | flops 20464 | bytes 16520 | tf_op jit(solution)/shard_map/reduce_sum | solution.py:306
  11.8 1.5 %collective-permute-done.1.high_ref = bf16[2,160,256]{2,1,0:T(8,128)(2,1)S(1)} collective-permute-done((bf16[2,160,256]{2,1,0:T(8,128)(2,1)S(1)}, bf16[2,160,256]{2,1,0:T(8,128)(2,1)S(1)}, u32[]{:S(2)}, u32[]{:S(2)}) %collective-permute-start.1) | collective-permute-done | bytes 163872 | tf_op jit(solution)/shard_map/ppermute | solution.py:299
  13.2 1.3 %copy-done.2 = bf16[1,16,160,256]{3,2,1,0:T(8,128)(2,1)S(1)} copy-done((bf16[1,16,160,256]{3,2,1,0:T(8,128)(2,1)S(1)}, bf16[1,16,160,256]{3,2,1,0:T(8,128)(2,1)}, u32[]{:S(2)}) %copy-start.2) | copy-done | bytes 1310744
  14.5 1.3 %copy-done.4 = bf16[3,3,256,256]{3,2,1,0:T(8,128)(2,1)S(1)} copy-done((bf16[3,3,256,256]{3,2,1,0:T(8,128)(2,1)S(1)}, bf16[3,3,256,256]{3,2,1,0:T(8,128)(2,1)}, u32[]{:S(2)}) %copy-start.4) | copy-done | bytes 1179672
  15.8 1.3 %copy-done.5 = bf16[3,3,256,256]{3,2,1,0:T(8,128)(2,1)S(1)} copy-done((bf16[3,3,256,256]{3,2,1,0:T(8,128)(2,1)S(1)}, bf16[3,3,256,256]{3,2,1,0:T(8,128)(2,1)}, u32[]{:S(2)}) %copy-start.5) | copy-done | bytes 1179672
  17.1 0.7 copy-done.6
  19.1 9.7 %convs.1 = (bf16[16,160,256]{2,1,0:T(8,128)(2,1)}, bf16[16,40,256]{2,1,0:T(8,128)(2,1)}) custom-call(s32[16]{0:T(128)S(1)} %select_reduce_fusion.pick_ref, f32[2]{0:T(128)S(1)} %add_convert_fusion.edge_ref, bf16[16,160,256]{2,1,0:T(8,128)(2,1)S(1)} %bitcast.29, bf16[2,160,256]{2,1,0:T(8,128)(2,1)S(1)} %collective-permute-done.low_ref, ...), custom_call_target="tpu_custom_call" | custom-call | flops 6417285120 | bytes 6291456 | tf_op jit(solution)/shard_map/convs/pallas_call | solution.py:110
  28.8 6.8 %all-to-all-start = ((bf16[16,40,256]{2,1,0:T(8,128)(2,1)}), bf16[16,40,256]{2,1,0:T(8,128)(2,1)S(1)}, u32[]{:S(2)}, u32[]{:S(2)}) async-start(bf16[16,40,256]{2,1,0:T(8,128)(2,1)} %get-tuple-element.18), calls=%async_computation | async-start | bytes 655360 | tf_op jit(solution)/shard_map/all_to_all | solution.py:334
  35.9 7.4 %all-to-all-done.refs_2_ = bf16[16,40,256]{2,1,0:T(8,128)(2,1)S(1)} async-done(((bf16[16,40,256]{2,1,0:T(8,128)(2,1)}), bf16[16,40,256]{2,1,0:T(8,128)(2,1)S(1)}, u32[]{:S(2)}, u32[]{:S(2)}) %all-to-all-start) | async-done | bytes 327712 | tf_op jit(solution)/shard_map/all_to_all | solution.py:334
  43.2 2.8 %collective-permute-start.2 = (bf16[16,40,256]{2,1,0:T(8,128)(2,1)S(1)}, bf16[16,40,256]{2,1,0:T(8,128)(2,1)S(1)}, u32[]{:S(2)}, u32[]{:S(2)}) collective-permute-start(bf16[16,40,256]{2,1,0:T(8,128)(2,1)S(1)} %all-to-all-done.refs_2_), channel_id=1, source_target_pairs={{0,2},{1,3},{2,4},{3,5},{4,6},{5,7},{6,0},{7,1},{8,10},{9,11},{10,... | collective-permute-start | bytes 983048 | tf_op jit(solution)/shard_map/ppermute | solution.py:286
  46.1 1.1 %collective-permute-start.4 = (bf16[16,40,256]{2,1,0:T(8,128)(2,1)S(1)}, bf16[16,40,256]{2,1,0:T(8,128)(2,1)S(1)}, u32[]{:S(2)}, u32[]{:S(2)}) collective-permute-start(bf16[16,40,256]{2,1,0:T(8,128)(2,1)S(1)} %all-to-all-done.refs_2_), channel_id=1, source_target_pairs={{0,6},{1,7},{2,0},{3,1},{4,2},{5,3},{6,4},{7,5},{8,14},{9,15},{10,... | collective-permute-start | bytes 983048 | tf_op jit(solution)/shard_map/ppermute | solution.py:286
  48.5 6.8 %collective-permute-done.2.refs_2_ = bf16[16,40,256]{2,1,0:T(8,128)(2,1)S(1)} collective-permute-done((bf16[16,40,256]{2,1,0:T(8,128)(2,1)S(1)}, bf16[16,40,256]{2,1,0:T(8,128)(2,1)S(1)}, u32[]{:S(2)}, u32[]{:S(2)}) %collective-permute-start.2) | collective-permute-done | bytes 327712 | tf_op jit(solution)/shard_map/ppermute | solution.py:286
  55.4 2.7 %collective-permute-start.5 = (bf16[8,40,256]{2,1,0:T(8,128)(2,1)S(1)}, bf16[8,40,256]{2,1,0:T(8,128)(2,1)S(1)}, u32[]{:S(2)}, u32[]{:S(2)}) collective-permute-start(bf16[8,40,256]{2,1,0:T(8,128)(2,1)S(1)} %slice.49), channel_id=1, source_target_pairs={{0,6},{1,7},{2,0},{3,1},{4,2},{5,3},{6,4},{7,5},{8,14},{9,15},{10,... | collective-permute-start | bytes 491528 | tf_op jit(solution)/shard_map/ppermute | solution.py:286
  58.1 1.1 %collective-permute-start.8 = (bf16[16,40,256]{2,1,0:T(8,128)(2,1)S(1)}, bf16[16,40,256]{2,1,0:T(8,128)(2,1)S(1)}, u32[]{:S(2)}, u32[]{:S(2)}) collective-permute-start(bf16[16,40,256]{2,1,0:T(8,128)(2,1)S(1)} %collective-permute-done.2.refs_2_), channel_id=1, source_target_pairs={{0,1},{1,0},{2,3},{3,2},{4,5},{5,4},{6,7},{7,6},{8,9},{9,8},{10,11... | collective-permute-start | bytes 983048 | tf_op jit(solution)/shard_map/ppermute | solution.py:281
  59.3 3.5 %attend.4 = (f32[1280,128]{1,0:T(8,128)S(1)}, f32[1280,128]{1,0:T(8,128)S(1)}, f32[1280,256]{1,0:T(8,128)S(1)}) custom-call(bf16[1280,256]{1,0:T(8,128)(2,1)S(1)} %get-tuple-element.16.refs_0_, bf16[1280,256]{1,0:T(8,128)(2,1)S(1)} %get-tuple-element.17.refs_1_, bf16[16,40,256]{2,1,0:T(8,128)(2,1)S(1)} %all-to-all-done.refs_2_, ...), custom_call_target="tpu_custom_call" | custom-call | flops 2516582400 | bytes 6291456 | tf_op jit(solution)/shard_map/attend/pallas_call | solution.py:261
  62.8 4.0 %attend.5 = (f32[1280,128]{1,0:T(8,128)S(1)}, f32[1280,128]{1,0:T(8,128)S(1)}, f32[1280,256]{1,0:T(8,128)S(1)}) custom-call(bf16[1280,256]{1,0:T(8,128)(2,1)S(1)} %get-tuple-element.16.refs_0_, bf16[1280,256]{1,0:T(8,128)(2,1)S(1)} %get-tuple-element.17.refs_1_, ...), custom_call_target="tpu_custom_call", output_to_operand_aliasing={{0}: (5, {}), {1}: (6, {}), {2}: (7, {})} | custom-call | flops 2516582400 | bytes 6291456 | tf_op jit(solution)/shard_map/attend/pallas_call | solution.py:261
  67.7 4.0 %attend.6 = (f32[1280,128]{1,0:T(8,128)S(1)}, f32[1280,128]{1,0:T(8,128)S(1)}, f32[1280,256]{1,0:T(8,128)S(1)}) custom-call(bf16[1280,256]{1,0:T(8,128)(2,1)S(1)} %get-tuple-element.16.refs_0_, bf16[1280,256]{1,0:T(8,128)(2,1)S(1)} %get-tuple-element.17.refs_1_, ...), custom_call_target="tpu_custom_call", output_to_operand_aliasing={{0}: (5, {}), {1}: (6, {}), {2}: (7, {})} | custom-call | flops 2516582400 | bytes 6291456 | tf_op jit(solution)/shard_map/attend/pallas_call | solution.py:261
  71.7 5.2 %attend.7 = bf16[64,2560]{1,0:T(8,128)(2,1)} custom-call(bf16[1280,256]{1,0:T(8,128)(2,1)S(1)} %get-tuple-element.16.refs_0_, bf16[1280,256]{1,0:T(8,128)(2,1)S(1)} %get-tuple-element.17.refs_1_, bf16[8,40,256]{2,1,0:T(8,128)(2,1)S(1)} %collective-permute-done.3.refs_2_, bf16[8,40,256]{2,1,0:T(8,128)(2,1)S(1)} %collective-permute-done.5.refs_3_, ...), custom_call_target="tpu_custom_call" | custom-call | flops 2516582400 | bytes 6291456 | tf_op jit(solution)/shard_map/attend/pallas_call | solution.py:261
  (47 shorter events, 4.1 us)
Async XLA Ops:
  1.7 10.1 %collective-permute-start = (bf16[2,160,256]{2,1,0:T(8,128)(2,1)S(1)}, bf16[2,160,256]{2,1,0:T(8,128)(2,1)S(1)}, u32[]{:S(2)}, u32[]{:S(2)}) collective-permute-start(bf16[2,160,256]{2,1,0:T(8,128)(2,1)S(1)} %get-tuple-element.29), channel_id=1, source_target_pairs={{0,1},{1,2},{2,3},{3,4},{4,5},{5,6},{6,7},{8,9},{9,10},{10,11},{11... | collective-permute-start | bytes 491528 | tf_op jit(solution)/shard_map/ppermute | solution.py:298
  6.6 6.6 %collective-permute-start.1 = (bf16[2,160,256]{2,1,0:T(8,128)(2,1)S(1)}, bf16[2,160,256]{2,1,0:T(8,128)(2,1)S(1)}, u32[]{:S(2)}, u32[]{:S(2)}) collective-permute-start(bf16[2,160,256]{2,1,0:T(8,128)(2,1)S(1)} %get-tuple-element.28), channel_id=1, source_target_pairs={{1,0},{2,1},{3,2},{4,3},{5,4},{6,5},{7,6},{9,8},{10,9},{11,10},{12... | collective-permute-start | bytes 491528 | tf_op jit(solution)/shard_map/ppermute | solution.py:299
  13.2 1.3 %copy-start.2 = (bf16[1,16,160,256]{3,2,1,0:T(8,128)(2,1)S(1)}, bf16[1,16,160,256]{3,2,1,0:T(8,128)(2,1)}, u32[]{:S(2)}) copy-start(bf16[1,16,160,256]{3,2,1,0:T(8,128)(2,1)} %param.12) | copy-start | bytes 3932164
  14.5 1.3 %copy-start.4 = (bf16[3,3,256,256]{3,2,1,0:T(8,128)(2,1)S(1)}, bf16[3,3,256,256]{3,2,1,0:T(8,128)(2,1)}, u32[]{:S(2)}) copy-start(bf16[3,3,256,256]{3,2,1,0:T(8,128)(2,1)} %param.13) | copy-start | bytes 3538948
  15.8 1.3 %copy-start.5 = (bf16[3,3,256,256]{3,2,1,0:T(8,128)(2,1)S(1)}, bf16[3,3,256,256]{3,2,1,0:T(8,128)(2,1)}, u32[]{:S(2)}) copy-start(bf16[3,3,256,256]{3,2,1,0:T(8,128)(2,1)} %param.14) | copy-start | bytes 3538948
  17.1 0.7 copy-start.6
  17.8 0.7 copy-start.7
  18.4 0.7 copy-start.8
  19.1 28.8 %copy-start = (bf16[256,2560]{1,0:T(8,128)(2,1)S(1)}, bf16[256,2560]{1,0:T(8,128)(2,1)}, u32[]{:S(2)}) copy-start(bf16[256,2560]{1,0:T(8,128)(2,1)} %wk_ref.1) | copy-start | bytes 3932164
  19.1 28.8 %copy-start.1 = (bf16[64,2560]{1,0:T(8,128)(2,1)S(1)}, bf16[64,2560]{1,0:T(8,128)(2,1)}, u32[]{:S(2)}) copy-start(bf16[64,2560]{1,0:T(8,128)(2,1)} %q_ref.1) | copy-start | bytes 983044
  28.8 14.4 %all-to-all-start = ((bf16[16,40,256]{2,1,0:T(8,128)(2,1)}), bf16[16,40,256]{2,1,0:T(8,128)(2,1)S(1)}, u32[]{:S(2)}, u32[]{:S(2)}) async-start(bf16[16,40,256]{2,1,0:T(8,128)(2,1)} %get-tuple-element.18), calls=%async_computation | async-start | bytes 655360 | tf_op jit(solution)/shard_map/all_to_all | solution.py:334
  43.2 16.0 %collective-permute-start.10 = (bf16[16,40,256]{2,1,0:T(8,128)(2,1)S(1)}, bf16[16,40,256]{2,1,0:T(8,128)(2,1)S(1)}, u32[]{:S(2)}, u32[]{:S(2)}) collective-permute-start(bf16[16,40,256]{2,1,0:T(8,128)(2,1)S(1)} %all-to-all-done.refs_2_), channel_id=1, source_target_pairs={{0,1},{1,0},{2,3},{3,2},{4,5},{5,4},{6,7},{7,6},{8,9},{9,8},{10,11... | collective-permute-start | bytes 983048 | tf_op jit(solution)/shard_map/ppermute | solution.py:281
  43.2 12.0 %collective-permute-start.2 = (bf16[16,40,256]{2,1,0:T(8,128)(2,1)S(1)}, bf16[16,40,256]{2,1,0:T(8,128)(2,1)S(1)}, u32[]{:S(2)}, u32[]{:S(2)}) collective-permute-start(bf16[16,40,256]{2,1,0:T(8,128)(2,1)S(1)} %all-to-all-done.refs_2_), channel_id=1, source_target_pairs={{0,2},{1,3},{2,4},{3,5},{4,6},{5,7},{6,0},{7,1},{8,10},{9,11},{10,... | collective-permute-start | bytes 983048 | tf_op jit(solution)/shard_map/ppermute | solution.py:286
  46.1 9.3 %collective-permute-start.4 = (bf16[16,40,256]{2,1,0:T(8,128)(2,1)S(1)}, bf16[16,40,256]{2,1,0:T(8,128)(2,1)S(1)}, u32[]{:S(2)}, u32[]{:S(2)}) collective-permute-start(bf16[16,40,256]{2,1,0:T(8,128)(2,1)S(1)} %all-to-all-done.refs_2_), channel_id=1, source_target_pairs={{0,6},{1,7},{2,0},{3,1},{4,2},{5,3},{6,4},{7,5},{8,14},{9,15},{10,... | collective-permute-start | bytes 983048 | tf_op jit(solution)/shard_map/ppermute | solution.py:286
  55.3 11.4 %collective-permute-start.3 = (bf16[8,40,256]{2,1,0:T(8,128)(2,1)S(1)}, bf16[8,40,256]{2,1,0:T(8,128)(2,1)S(1)}, u32[]{:S(2)}, u32[]{:S(2)}) collective-permute-start(bf16[8,40,256]{2,1,0:T(8,128)(2,1)S(1)} %slice.48), channel_id=1, source_target_pairs={{0,2},{1,3},{2,4},{3,5},{4,6},{5,7},{6,0},{7,1},{8,10},{9,11},{10,... | collective-permute-start | bytes 491528 | tf_op jit(solution)/shard_map/ppermute | solution.py:286
  55.4 11.9 %collective-permute-start.5 = (bf16[8,40,256]{2,1,0:T(8,128)(2,1)S(1)}, bf16[8,40,256]{2,1,0:T(8,128)(2,1)S(1)}, u32[]{:S(2)}, u32[]{:S(2)}) collective-permute-start(bf16[8,40,256]{2,1,0:T(8,128)(2,1)S(1)} %slice.49), channel_id=1, source_target_pairs={{0,6},{1,7},{2,0},{3,1},{4,2},{5,3},{6,4},{7,5},{8,14},{9,15},{10,... | collective-permute-start | bytes 491528 | tf_op jit(solution)/shard_map/ppermute | solution.py:286
  58.1 9.5 %collective-permute-start.8 = (bf16[16,40,256]{2,1,0:T(8,128)(2,1)S(1)}, bf16[16,40,256]{2,1,0:T(8,128)(2,1)S(1)}, u32[]{:S(2)}, u32[]{:S(2)}) collective-permute-start(bf16[16,40,256]{2,1,0:T(8,128)(2,1)S(1)} %collective-permute-done.2.refs_2_), channel_id=1, source_target_pairs={{0,1},{1,0},{2,3},{3,2},{4,5},{5,4},{6,7},{7,6},{8,9},{9,8},{10,11... | collective-permute-start | bytes 983048 | tf_op jit(solution)/shard_map/ppermute | solution.py:281
  59.3 8.4 %collective-permute-start.9 = (bf16[16,40,256]{2,1,0:T(8,128)(2,1)S(1)}, bf16[16,40,256]{2,1,0:T(8,128)(2,1)S(1)}, u32[]{:S(2)}, u32[]{:S(2)}) collective-permute-start(bf16[16,40,256]{2,1,0:T(8,128)(2,1)S(1)} %collective-permute-done.4.refs_3_), channel_id=1, source_target_pairs={{0,1},{1,0},{2,3},{3,2},{4,5},{5,4},{6,7},{7,6},{8,9},{9,8},{10,11... | collective-permute-start | bytes 983048 | tf_op jit(solution)/shard_map/ppermute | solution.py:281
  66.7 4.9 %collective-permute-start.6 = (bf16[8,40,256]{2,1,0:T(8,128)(2,1)S(1)}, bf16[8,40,256]{2,1,0:T(8,128)(2,1)S(1)}, u32[]{:S(2)}, u32[]{:S(2)}) collective-permute-start(bf16[8,40,256]{2,1,0:T(8,128)(2,1)S(1)} %collective-permute-done.3.refs_2_), channel_id=1, source_target_pairs={{0,1},{1,0},{2,3},{3,2},{4,5},{5,4},{6,7},{7,6},{8,9},{9,8},{10,11... | collective-permute-start | bytes 491528 | tf_op jit(solution)/shard_map/ppermute | solution.py:281
  67.3 4.3 %collective-permute-start.7 = (bf16[8,40,256]{2,1,0:T(8,128)(2,1)S(1)}, bf16[8,40,256]{2,1,0:T(8,128)(2,1)S(1)}, u32[]{:S(2)}, u32[]{:S(2)}) collective-permute-start(bf16[8,40,256]{2,1,0:T(8,128)(2,1)S(1)} %collective-permute-done.5.refs_3_), channel_id=1, source_target_pairs={{0,1},{1,0},{2,3},{3,2},{4,5},{5,4},{6,7},{7,6},{8,9},{9,8},{10,11... | collective-permute-start | bytes 491528 | tf_op jit(solution)/shard_map/ppermute | solution.py:281
  67.7 4.0 %copy-start.3 = (bf16[256,2560]{1,0:T(8,128)(2,1)S(1)}, bf16[256,2560]{1,0:T(8,128)(2,1)}, u32[]{:S(2)}) copy-start(bf16[256,2560]{1,0:T(8,128)(2,1)} %refs_10_.1) | copy-start | bytes 3932164

commit v2 on v1

v2 whole, which is shorter than its diff:
```python
import functools

import jax
import jax.numpy as jnp
from jax import lax
from jax.experimental import pallas as pl
from jax.experimental.pallas import tpu as pltpu
from jax.sharding import PartitionSpec as P

C = 256
HEADS = 20
HD = 128
QW = 4
BT = 40
W = 160
ROWS = 16
Q_DEV = 64
FRAMES = 16
TILES = 8
QROWS = HEADS * Q_DEV
EPSILON = 1e-06
NEGATIVE = -1e30
LOG2E = 1.4426950408889634
VMEM = pl.BlockSpec(memory_space=pltpu.VMEM)
SMEM = pl.BlockSpec(memory_space=pltpu.SMEM)


def normalized(wide, gain):
    mean_square = jnp.mean(wide * wide, axis=-1, keepdims=True)
    return wide * lax.rsqrt(mean_square + EPSILON) * gain


def store_windows(act, dst_ref, row):
    column = lax.broadcasted_iota(jnp.int32, (8, C), 0)
    left = pltpu.roll(act, 1, 0)
    left = jnp.concatenate([jnp.where(column == 0, 0.0, left[:8]), left[8:]], 0)
    right = pltpu.roll(act, W - 1, 0)
    right = jnp.concatenate([right[: W - 8], jnp.where(column == 7, 0.0, right[W - 8 :])], 0)
    dst_ref[row, :, 0:C] = left.astype(jnp.bfloat16)
    dst_ref[row, :, C : 2 * C] = act.astype(jnp.bfloat16)
    dst_ref[row, :, 2 * C : 3 * C] = right.astype(jnp.bfloat16)


def silu_norm(wide, half_gain):
    half = normalized(wide, half_gain)
    return half + half * jnp.tanh(half)


def dot_rows(windows, weight_ref):
    total = None
    for step, window in enumerate(windows):
        part = jnp.dot(
            window.reshape(-1, 3 * C), weight_ref[step], preferred_element_type=jnp.float32
        )
        total = part if total is None else total + part
    return total


INNER = ROWS - 2


def inner_kernel(
    x_hbm, w1_hbm, w2_hbm, g1_hbm, g2_hbm, gk_hbm, frames_hbm, blocks_hbm,
    second_ref, middle_ref, sides_ref, base_ref, w1_ref, w2_ref,
    g1_ref, g2_ref, gk_ref, frames_ref, blocks_ref,
    x_ref, first_ref, sems,
):
    chunk = ROWS // 4
    pairs = [(g1_hbm, g1_ref), (g2_hbm, g2_ref)]
    for k in range(4):
        own = pl.ds(k * chunk, chunk)
        pairs.append((x_hbm.at[own], x_ref.at[own]))
    pairs += [
        (w1_hbm, w1_ref), (w2_hbm, w2_ref), (gk_hbm, gk_ref),
        (frames_hbm, frames_ref), (blocks_hbm, blocks_ref),
    ]
    copies = [
        pltpu.make_async_copy(src, dst, sems.at[k]) for k, (src, dst) in enumerate(pairs)
    ]
    for copy in copies:
        copy.start()
    copies[0].wait()
    copies[1].wait()
    g1 = g1_ref[...] * 0.5
    g2 = g2_ref[...] * 0.5

    def first_rows(rows):
        for row in rows:
            store_windows(silu_norm(x_ref[row].astype(jnp.float32), g1), first_ref, row)

    def middle_rows(rows):
        start, count = rows[0], len(rows)
        return dot_rows(
            [first_ref[start + step : start + step + count] for step in range(3)], w1_ref
        )

    def second_rows(rows, total):
        for k, row in enumerate(rows):
            middle = x_ref[row + 1].astype(jnp.float32) + total[k * W : (k + 1) * W]
            middle_ref[row] = middle.astype(jnp.bfloat16)
            store_windows(silu_norm(middle, g2), second_ref, row)

    copies[2].wait()
    first_rows(range(0, chunk))
    for copy in copies[3:]:
        copy.wait()
    first_rows(range(chunk, 7))
    parts = [range(0, 5), range(5, 10), range(10, INNER)]
    totals = [middle_rows(parts[0])]
    first_rows(range(7, 12))
    totals.append(middle_rows(parts[1]))
    first_rows(range(12, ROWS))
    second_rows(parts[0], totals[0])
    totals.append(middle_rows(parts[2]))
    for k in range(2):
        sides_ref[k] = first_ref[k]
        sides_ref[2 + k] = first_ref[ROWS - 2 + k]
        base_ref[k] = x_ref[k * (ROWS - 1)]
    second_rows(parts[1], totals[1])
    second_rows(parts[2], totals[2])


def inner_call(latents, w1, w2, g1, g2, gk, frame_ids, block_ids):
    weight = jax.ShapeDtypeStruct((3, 3 * C, C), jnp.bfloat16)
    gain = jax.ShapeDtypeStruct((1, C), jnp.float32)
    table = jax.ShapeDtypeStruct(frame_ids.shape, jnp.int32)
    out_shape = (
        jax.ShapeDtypeStruct((INNER, W, 3 * C), jnp.bfloat16),
        jax.ShapeDtypeStruct((INNER, W, C), jnp.bfloat16),
        jax.ShapeDtypeStruct((4, W, 3 * C), jnp.bfloat16),
        jax.ShapeDtypeStruct((2, W, C), jnp.bfloat16),
        weight, weight, gain, gain, gain, table, table,
    )
    return pl.pallas_call(
        inner_kernel,
        name="inner_rows",
        out_shape=out_shape,
        in_specs=[pl.BlockSpec(memory_space=pltpu.HBM)] * 8,
        out_specs=(VMEM,) * len(out_shape),
        scratch_shapes=[
            pltpu.VMEM((ROWS, W, C), jnp.bfloat16),
            pltpu.VMEM((ROWS, W, 3 * C), jnp.bfloat16),
            pltpu.SemaphoreType.DMA((11,)),
        ],
        compiler_params=pltpu.CompilerParams(vmem_limit_bytes=28 * 1024 * 1024),
        cost_estimate=pl.CostEstimate(
            flops=2 * 9 * C * C * W * INNER, bytes_accessed=4 << 20, transcendentals=0
        ),
    )(latents, w1, w2, g1, g2, gk, frame_ids, block_ids)


def outer_kernel(
    near_ref, away_ref, inner_ref, middle_ref, sides_ref, base_ref, w1_ref, w2_ref,
    g1_ref, g2_ref, gk_ref, frames_ref, blocks_ref,
    refined_hbm, picked_ref,
    refined_ref, first_ref, side_middle_ref, second_ref, wide_ref, sems,
):
    frame = lax.axis_index("frames")
    tile = lax.axis_index("tile")
    north = lax.rem(tile, 2) == 1
    half = (ROWS - 4) // 2
    total = dot_rows([inner_ref[step : step + half] for step in range(3)], w2_ref)

    per_tile = ROWS * QW
    own = blocks_ref[...] - tile * per_tile
    hit = (frames_ref[...] == frame) & (own >= 0) & (own < per_tile)
    found = jnp.where(hit, own, 0).astype(jnp.float32)
    picks = [jnp.max(found[g : g + 1]).astype(jnp.int32) for g in range(FRAMES)]

    def second_rows(total, rows):
        for k, row in enumerate(rows):
            if 0 < row < ROWS - 1:
                base = middle_ref[row - 1]
            else:
                base = side_middle_ref[1 if row == 0 else 2]
            out = base.astype(jnp.float32) + total[k * W : (k + 1) * W]
            out = out.astype(jnp.bfloat16)
            refined_ref[row] = out
            wide_ref[row * W : (row + 1) * W] = out.astype(jnp.float32)

    def send(k, start, count):
        rows = pl.ds(start, count)
        copy = pltpu.make_async_copy(refined_ref.at[rows], refined_hbm.at[rows], sems.at[k])
        copy.start()
        return copy

    g1 = g1_ref[...] * 0.5
    g2 = g2_ref[...] * 0.5
    low, high = [], []
    for k in range(2):
        near = near_ref[k].astype(jnp.float32)
        away = away_ref[k].astype(jnp.float32)
        low.append(jnp.where(north, near, away))
        high.append(jnp.where(north, away, near))
    for k in range(2):
        store_windows(silu_norm(low[k], g1), first_ref, k)
        first_ref[2 + k] = sides_ref[k]
        first_ref[4 + k] = sides_ref[2 + k]
        store_windows(silu_norm(high[k], g1), first_ref, 6 + k)
        second_ref[2 + k] = inner_ref[k]
        second_ref[4 + k] = inner_ref[INNER - 2 + k]
    edges = dot_rows(
        [
            jnp.concatenate([first_ref[step : step + 2], first_ref[4 + step : 6 + step]], 0)
            for step in range(3)
        ],
        w1_ref,
    )
    second_rows(total, range(2, 2 + half))
    total = dot_rows([inner_ref[half + step : 2 * half + step] for step in range(3)], w2_ref)

    bases = [low[1], base_ref[0].astype(jnp.float32), base_ref[1].astype(jnp.float32), high[0]]
    places = [0, 1, 6, 7]
    for k in range(4):
        middle = bases[k] + edges[k * W : (k + 1) * W]
        act = silu_norm(middle, g2)
        if k == 0:
            act = jnp.where(tile > 0, act, 0.0)
        if k == 3:
            act = jnp.where(tile < TILES - 1, act, 0.0)
        side_middle_ref[k] = middle.astype(jnp.bfloat16)
        store_windows(act, second_ref, places[k])
    edges = dot_rows(
        [
            jnp.concatenate([second_ref[step : step + 2], second_ref[4 + step : 6 + step]], 0)
            for step in range(3)
        ],
        w2_ref,
    )
    second_rows(total, range(2 + half, ROWS - 2))
    second_rows(edges, [0, 1, ROWS - 2, ROWS - 1])
    copy = send(0, 0, ROWS)

    gk = gk_ref[...]
    for g in range(FRAMES):
        at = pl.multiple_of(picks[g] * BT, 8)
        block = normalized(wide_ref[pl.ds(at, BT)], gk)
        picked_ref[g] = block.astype(jnp.bfloat16)
    copy.wait()


def outer_call(near, away, inner):
    return pl.pallas_call(
        outer_kernel,
        name="outer_rows",
        out_shape=(
            jax.ShapeDtypeStruct((ROWS, W, C), jnp.bfloat16),
            jax.ShapeDtypeStruct((FRAMES, BT, C), jnp.bfloat16),
        ),
        in_specs=[VMEM] * 13,
        out_specs=(pl.BlockSpec(memory_space=pltpu.HBM), VMEM),
        scratch_shapes=[
            pltpu.VMEM((ROWS, W, C), jnp.bfloat16),
            pltpu.VMEM((8, W, 3 * C), jnp.bfloat16),
            pltpu.VMEM((4, W, C), jnp.bfloat16),
            pltpu.VMEM((8, W, 3 * C), jnp.bfloat16),
            pltpu.VMEM((ROWS * W, C), jnp.float32),
            pltpu.SemaphoreType.DMA((1,)),
        ],
        compiler_params=pltpu.CompilerParams(vmem_limit_bytes=28 * 1024 * 1024),
        cost_estimate=pl.CostEstimate(
            flops=2 * 9 * C * C * W * (ROWS + 4), bytes_accessed=4 << 20, transcendentals=0
        ),
    )(near, away, *inner)


def query_kernel(q_ref, wk_ref, frames_ref, blocks_ref, high_ref, low_ref, bias_ref):
    frame = lax.axis_index("frames")
    tile = lax.axis_index("tile")
    per_tile = ROWS * QW
    row = lax.broadcasted_iota(jnp.int32, frames_ref.shape, 0)
    source = frames_ref[...] * TILES + lax.shift_right_arithmetic(blocks_ref[...], 6)
    source = jnp.where((row == frame) & (frames_ref[...] >= 0), source, -1)
    source = jnp.max(source.astype(jnp.float32), axis=0, keepdims=True)
    sources = FRAMES * TILES
    number = lax.broadcasted_iota(jnp.int32, (sources, source.shape[1]), 0).astype(jnp.float32)
    listed = jnp.max(jnp.where(source == number, 1.0, 0.0), axis=1, keepdims=True)
    tokens = FRAMES * BT
    place = lax.broadcasted_iota(jnp.int32, (sources, tokens), 1)
    of_frame = lax.shift_right_logical(place * 205, 13)
    number = lax.broadcasted_iota(jnp.int32, (sources, tokens), 0)
    wide = jnp.broadcast_to(listed, (sources, tokens))
    depth, core = lax.div(tile, 2), lax.rem(tile, 2)
    odd = lax.rem(depth, 2) == 1
    even_side = jnp.where(odd, depth - 1, depth + 1)
    odd_side = lax.rem(jnp.where(odd, depth + 1, depth + 3), 4)
    planes = {"own": depth, "x": even_side, "y": odd_side, "far": lax.rem(depth + 2, 4)}
    for k, (plane, other) in enumerate(ORDER):
        at = 2 * planes[plane] + (1 - core if other else core)
        match = jnp.where(number == of_frame * TILES + at, wide, 0.0)
        there = jnp.max(match, axis=0, keepdims=True)
        bias_ref[k : k + 1] = jnp.where(there > 0.5, 0.0, NEGATIVE)

    scale = LOG2E / HD**0.5
    for h in range(HEADS):
        cols = slice(h * HD, (h + 1) * HD)
        turned = lax.dot_general(
            q_ref[:, cols], wk_ref[:, cols], (((1,), (1,)), ((), ())),
            preferred_element_type=jnp.float32,
        ) * scale
        high = turned.astype(jnp.bfloat16)
        high_ref[h * Q_DEV : (h + 1) * Q_DEV] = high
        low_ref[h * Q_DEV : (h + 1) * Q_DEV] = (turned - high.astype(jnp.float32)).astype(
            jnp.bfloat16
        )


ORDER = (
    ("own", 0), ("own", 1), ("x", 0), ("y", 0), ("x", 1), ("y", 1), ("far", 0), ("far", 1),
)


def query_call(queries, key_weight, frame_ids, block_ids):
    shape = jax.ShapeDtypeStruct((QROWS, C), jnp.bfloat16)
    return pl.pallas_call(
        query_kernel,
        name="turn_queries",
        out_shape=(shape, shape, jax.ShapeDtypeStruct((TILES, FRAMES * BT), jnp.float32)),
        in_specs=[VMEM] * 4,
        out_specs=(VMEM,) * 3,
        compiler_params=pltpu.CompilerParams(vmem_limit_bytes=16 * 1024 * 1024),
        cost_estimate=pl.CostEstimate(
            flops=2 * QROWS * HD * C, bytes_accessed=3 << 20, transcendentals=0
        ),
    )(queries, key_weight, frame_ids, block_ids)


BLOCK = 320
SLAB = 32


def attend_kernel(first, last, parts, chunk, *refs):
    refs = list(refs)
    qh_ref, ql_ref = refs[:2]
    x_refs = refs[2 : 2 + parts]
    bias_ref = refs[2 + parts]
    refs = refs[3 + parts :]
    if not first:
        m_in, l_in, acc_in = refs[:3]
        refs = refs[3:]
    if last:
        wv_ref, out_ref = refs[:2]
        refs = refs[2:]
    else:
        m_out, l_out, acc_out = refs[:3]
        refs = refs[3:]
    x_ref, s_ref, p_ref = refs
    tokens = x_ref.shape[0]
    at = 0
    for part in x_refs:
        size = part.shape[0] * part.shape[1]
        x_ref[at : at + size] = part[...].reshape(size, C)
        at += size
    bias = jnp.concatenate([bias_ref[2 * chunk : 2 * chunk + 1], bias_ref[2 * chunk + 1 : 2 * chunk + 2]], 1)

    def scores(block, slot):
        rows = slice(block * BLOCK, (block + 1) * BLOCK)
        dims = (((1,), (1,)), ((), ()))
        s_ref[slot] = lax.dot_general(
            qh_ref[rows], x_ref[...], dims, preferred_element_type=jnp.float32
        ) + lax.dot_general(ql_ref[rows], x_ref[...], dims, preferred_element_type=jnp.float32)

    blocks = QROWS // BLOCK
    scores(0, 0)
    for block in range(blocks):
        slot = block % 2
        if block + 1 < blocks:
            scores(block + 1, 1 - slot)
        alphas = []
        sums = []
        for slab in range(BLOCK // SLAB):
            own = slice(slab * SLAB, (slab + 1) * SLAB)
            rows = slice(block * BLOCK + slab * SLAB, block * BLOCK + (slab + 1) * SLAB)
            s = s_ref[slot, own] + bias
            peak = jnp.max(s, axis=-1, keepdims=True)
            if not first:
                old = m_in[rows, 0:1]
                peak = jnp.maximum(peak, old)
                alphas.append(jnp.exp2(old - peak))
            p = jnp.exp2(s - peak)
            total = jnp.sum(p, axis=-1, keepdims=True)
            if not first:
                total = total + alphas[-1] * l_in[rows, 0:1]
            p_ref[slot, own] = p.astype(jnp.bfloat16)
            if last:
                sums.append(total)
            else:
                m_out[rows] = jnp.broadcast_to(peak, (SLAB, 128))
                l_out[rows] = jnp.broadcast_to(total, (SLAB, 128))
        rows = slice(block * BLOCK, (block + 1) * BLOCK)
        mixed = jnp.dot(p_ref[slot], x_ref[...], preferred_element_type=jnp.float32)
        if not first:
            mixed = mixed + jnp.concatenate(alphas, 0) * acc_in[rows]
        if not last:
            acc_out[rows] = mixed
        else:
            mixed = mixed / jnp.concatenate(sums, 0)
            high = mixed.astype(jnp.bfloat16)
            low = (mixed - high.astype(jnp.float32)).astype(jnp.bfloat16)
            for k in range(BLOCK // Q_DEV):
                h = block * (BLOCK // Q_DEV) + k
                cols = slice(h * HD, (h + 1) * HD)
                own = slice(k * Q_DEV, (k + 1) * Q_DEV)
                both = jnp.concatenate([high[own], low[own]], 0)
                value = jnp.dot(both, wv_ref[:, cols], preferred_element_type=jnp.float32)
                out_ref[:, cols] = (value[:Q_DEV] + value[Q_DEV:]).astype(jnp.bfloat16)


def attend_call(qh, ql, parts, bias, chunk, state=None, value_weight=None):
    first = state is None
    last = value_weight is not None
    tokens = sum(part.shape[0] * part.shape[1] for part in parts)
    operands = [qh, ql, *parts, bias]
    aliases = {}
    if not first:
        if not last:
            aliases = {len(operands) + k: k for k in range(3)}
        operands += list(state)
    if last:
        operands.append(value_weight)
        out_shape = jax.ShapeDtypeStruct((Q_DEV, HEADS * HD), jnp.bfloat16)
        out_specs = VMEM
    else:
        stat = jax.ShapeDtypeStruct((QROWS, 128), jnp.float32)
        out_shape = (stat, stat, jax.ShapeDtypeStruct((QROWS, C), jnp.float32))
        out_specs = (VMEM, VMEM, VMEM)
    return pl.pallas_call(
        functools.partial(attend_kernel, first, last, len(parts), chunk),
        name="attend",
        out_shape=out_shape,
        in_specs=[VMEM] * len(operands),
        out_specs=out_specs,
        input_output_aliases=aliases,
        scratch_shapes=[
            pltpu.VMEM((tokens, C), jnp.bfloat16),
            pltpu.VMEM((2, BLOCK, tokens), jnp.float32),
            pltpu.VMEM((2, BLOCK, tokens), jnp.bfloat16),
        ],
        compiler_params=pltpu.CompilerParams(vmem_limit_bytes=40 * 1024 * 1024),
        cost_estimate=pl.CostEstimate(
            flops=6 * QROWS * C * tokens, bytes_accessed=6 << 20, transcendentals=QROWS * tokens
        ),
    )(*operands)


def core_swap(x):
    return lax.ppermute(x, "tile", [(t, t ^ 1) for t in range(TILES)])


def partner_plane(z, odd):
    return z ^ 1 if not odd else ((z + 1) % 4 if z % 2 else (z + 3) % 4)


def plane_swap(x, odds):
    pairs = [(t, 2 * partner_plane(t // 2, odds[t % 2]) + t % 2) for t in range(TILES)]
    return lax.ppermute(x, "tile", pairs)


def local(
    latents, conv_first, conv_second, gain_first, gain_second, gain_key,
    queries, key_weight, value_weight, frame_ids, block_ids, counts,
):
    core = lax.rem(lax.axis_index("tile"), 2)
    own = latents[0]
    near = lax.dynamic_slice_in_dim(own, (ROWS - 2) * (1 - core), 2, 0)
    away = lax.dynamic_slice_in_dim(own, (ROWS - 2) * core, 2, 0)
    near = core_swap(near)
    across = [(t, t + 1 if t % 2 else t - 1) for t in range(1, TILES - 1)]
    away = lax.ppermute(away, "tile", across)

    stay = functools.partial(pltpu.with_memory_space_constraint, memory_space=pltpu.HBM)
    inner = inner_call(
        stay(own),
        stay(conv_first.reshape(3, 3 * C, C)), stay(conv_second.reshape(3, 3 * C, C)),
        stay(gain_first[None]), stay(gain_second[None]), stay(gain_key[None]),
        stay(frame_ids), stay(block_ids),
    )
    refined, picked = outer_call(near, away, inner)
    qh, ql, bias = query_call(queries, key_weight, inner[9], inner[10])
    mine = lax.all_to_all(picked, "frames", split_axis=0, concat_axis=0, tiled=True)
    partner = core_swap(mine)
    even_side = plane_swap(mine, (False, False))
    odd_side = plane_swap(mine, (True, True))
    state = attend_call(qh, ql, (mine, partner), bias, 0)
    even_side, odd_side, state = lax.optimization_barrier((even_side, odd_side, state))
    far = plane_swap(jnp.where(core == 0, even_side, odd_side), (True, False))
    even_swap = core_swap(even_side)
    odd_swap = core_swap(odd_side)
    state = attend_call(qh, ql, (even_side, odd_side), bias, 1, state)
    far, state = lax.optimization_barrier((far, state))
    far_swap = core_swap(far)
    state = attend_call(qh, ql, (even_swap, odd_swap), bias, 2, state)
    attended = attend_call(qh, ql, (far, far_swap), bias, 3, state, value_weight)
    return (refined[None], attended)


def solution(mesh):
    in_specs = (
        P("frames", "tile", None, None),
        P(), P(), P(), P(), P(),
        P(("frames", "tile"), None),
        P(), P(), P(), P(), P(),
    )
    out_specs = (P("frames", "tile", None, None), P(("frames", "tile"), None))
    return jax.shard_map(local, mesh=mesh, in_specs=in_specs, out_specs=out_specs, check_vma=False)
```

time: 77.4 us -> 65.3 us (0.84)
  blocking collectives: 0 us -> 14.4 us
  waiting for transfers between devices: 15.6 us -> 3.51 us
  local copies, waits for them, and re-layouts: 8.4 us -> 1.04 us
  starting transfers between devices: 22.4 us -> 15.7 us
  Pallas kernels: 26.9 us -> 29.7 us
  other arithmetic: 2.72 us -> 0.04 us
    all_to_all x0 -> x1, blocking collectives: none -> 14.4 us  [local(): lax.all_to_all(picked, 'frames', split_axis=0, concat_axis=0, tiled=True)]
    all_to_all x1 -> x0, waiting for transfers between devices: 7.37 us -> none  [local(): lax.all_to_all(picked, 'frames', split_axis=0, concat_axis=0, tiled=True)]
    all_to_all x1 -> x0, starting transfers between devices: 6.75 us -> none  [local(): lax.all_to_all(picked, 'frames', split_axis=0, concat_axis=0, tiled=True)]
    unnamed x18 -> x6, local copies, waits for them, and re-layouts: 5.9 us -> 0.02 us
    ppermute x5, starting transfers between devices: 2.06 us -> 6.94 us  [core_swap(): return lax.ppermute(x, 'tile', [(t, t ^ 1) for t in range(TILES)])]
    ppermute x6 -> x4, starting transfers between devices: 13.6 us -> 8.75 us  [the longest x1 4.92 us: local(): away = lax.ppermute(away, 'tile', across)]
    ppermute x6 -> x4, waiting for transfers between devices: 8.25 us -> 3.5 us  [the longest x3 3.5 us: plane_swap(): return lax.ppermute(x, 'tile', pairs)]
    pallas_call x5 -> x6, Pallas kernels: 26.3 us -> 28.6 us  [the longest x4 17.2 us: attend_call(): pl.pallas_call(functools.partial(attend_kernel, first, last, len(parts),...]
  transfers between devices with their start and end apart: 12 -> 9, of which waited for: 3 -> 2; matrix products, arithmetic and copies ran while one was open for 5% -> 0% of each run, Pallas kernels for 16% -> 29%
where the time goes in v2:
time: 65.3 us; the launch traced here: 65.2 us
  Pallas kernels  29.7 us (45%)
  starting transfers between devices  15.7 us (24%)
  blocking collectives  14.4 us (22%)
  waiting for transfers between devices  3.51 us (5%)
  local copies, waits for them, and re-layouts  1.04 us (2%)
  between operations  0.78 us (1%)
    pallas_call x4, Pallas kernels, attend_call(): pl.pallas_call(functools.partial(attend_kernel, first, last, len(parts),...  17.2 us
    all_to_all x1, blocking collectives, local(): lax.all_to_all(picked, 'frames', split_axis=0, concat_axis=0, tiled=True)  14.4 us
    ppermute x5, starting transfers between devices, core_swap(): return lax.ppermute(x, 'tile', [(t, t ^ 1) for t in range(TILES)])  6.94 us
    pallas_call x1, Pallas kernels, inner_call(): pl.pallas_call(inner_kernel, name='inner_rows', out_shape=out_shape, in_s...  6.19 us
    pallas_call x1, Pallas kernels, outer_call(): pl.pallas_call(outer_kernel, name='outer_rows', out_shape=(jax.ShapeDtype...  5.15 us
    ppermute x1, starting transfers between devices, local(): away = lax.ppermute(away, 'tile', across)  4.92 us
    ppermute x3, starting transfers between devices, plane_swap(): return lax.ppermute(x, 'tile', pairs)  3.82 us
    ppermute x3, waiting for transfers between devices, plane_swap(): return lax.ppermute(x, 'tile', pairs)  3.5 us
  transfers between devices with their start and end apart: 9, of which 2 were waited for; matrix products, arithmetic and copies ran while one was open for 0% of the time, Pallas kernels for 29%

profile of v2, /device:TPU:1, one launch (start us, length us, event | category | flops | bytes accessed | tf_op | source)
XLA Modules:
  0.0 65.2 jit_solution(1928768476438834939)
XLA Ops:
  0.6 1.0 %dynamic-slice_bitcast_fusion = (bf16[2,160,256]{2,1,0:T(8,128)(2,1)S(1)}, bf16[2,160,256]{2,1,0:T(8,128)(2,1)S(1)}) fusion(bf16[1,16,160,256]{3,2,1,0:T(8,128)(2,1)} %param.12, s32[]{:T(128)S(6)} %select_n.15, s32[]{:T(128)S(6)} %select_n.14), kind=kLoop, calls=%fused_computation.1 | loop fusion | bytes 655368 | tf_op jit(solution)/shard_map/dynamic_slice | solution.py:466
  1.7 4.9 %collective-permute-start.1 = (bf16[2,160,256]{2,1,0:T(8,128)(2,1)S(1)}, bf16[2,160,256]{2,1,0:T(8,128)(2,1)S(1)}, u32[]{:S(2)}, u32[]{:S(2)}) collective-permute-start(bf16[2,160,256]{2,1,0:T(8,128)(2,1)S(1)} %get-tuple-element.70), channel_id=1, source_target_pairs={{1,2},{2,1},{3,4},{4,3},{5,6},{6,5},{9,10},{10,9},{11,12},{12,11},... | collective-permute-start | bytes 491528 | tf_op jit(solution)/shard_map/ppermute | solution.py:469
  6.6 0.1 collective-permute-start
  6.7 6.2 %inner_rows.1 = (bf16[14,160,768]{2,1,0:T(8,128)(2,1)S(1)}, bf16[14,160,256]{2,1,0:T(8,128)(2,1)S(1)}, bf16[4,160,768]{2,1,0:T(8,128)(2,1)S(1)}, bf16[2,160,256]...) custom-call(bf16[16,160,256]{2,1,0:T(8,128)(2,1)} %bitcast.11, ...), custom_call_target="tpu_custom_call" | custom-call | flops 2642411520 | bytes 4194304 | tf_op jit(solution)/shard_map/inner_rows/pallas_call | solution.py:134
  12.9 0.0 collective-permute-done.near_ref
  12.9 0.0 copy-start
  12.9 0.0 copy-start.1
  12.9 5.2 %outer_rows.1 = (bf16[16,160,256]{2,1,0:T(8,128)(2,1)}, bf16[16,40,256]{2,1,0:T(8,128)(2,1)S(1)}) custom-call(bf16[2,160,256]{2,1,0:T(8,128)(2,1)S(1)} %collective-permute-done.near_ref, bf16[2,160,256]{2,1,0:T(8,128)(2,1)S(1)} %collective-permute-done.1.away_ref, bf16[14,160,768]{2,1,0:T(8,128)(2,1)S(1)} %get-tuple-element.36.inner_ref, ...), custom_call_target="tpu_custom_call" | custom-call | flops 3774873600 | bytes 4194304 | tf_op jit(solution)/shard_map/outer_rows/pallas_call | solution.py:243
  18.1 14.4 %all_to_all.5.refs_2_ = bf16[16,40,256]{2,1,0:T(8,128)(2,1)S(1)} all-to-all(bf16[16,40,256]{2,1,0:T(8,128)(2,1)S(1)} %get-tuple-element.50), channel_id=1, replica_groups=mesh['frames'=16,'tile'=8] {'frames'}, dimensions={0} | all-to-all | bytes 655360 | tf_op jit(solution)/shard_map/all_to_all | solution.py:480
  32.5 2.3 %collective-permute-start.4 = (bf16[16,40,256]{2,1,0:T(8,128)(2,1)S(1)}, bf16[16,40,256]{2,1,0:T(8,128)(2,1)S(1)}, u32[]{:S(2)}, u32[]{:S(2)}) collective-permute-start(bf16[16,40,256]{2,1,0:T(8,128)(2,1)S(1)} %all_to_all.5.refs_2_), channel_id=1, source_target_pairs={{0,1},{1,0},{2,3},{3,2},{4,5},{5,4},{6,7},{7,6},{8,9},{9,8},{10,11... | collective-permute-start | bytes 983048 | tf_op jit(solution)/shard_map/ppermute | solution.py:447
  34.8 2.2 %collective-permute-start.3 = (bf16[16,40,256]{2,1,0:T(8,128)(2,1)S(1)}, bf16[16,40,256]{2,1,0:T(8,128)(2,1)S(1)}, u32[]{:S(2)}, u32[]{:S(2)}) collective-permute-start(bf16[16,40,256]{2,1,0:T(8,128)(2,1)S(1)} %all_to_all.5.refs_2_), channel_id=1, source_target_pairs={{0,6},{1,7},{2,4},{3,5},{4,2},{5,3},{6,0},{7,1},{8,14},{9,15},{10,... | collective-permute-start | bytes 983048 | tf_op jit(solution)/shard_map/ppermute | solution.py:456
  37.0 0.8 %collective-permute-start.2 = (bf16[16,40,256]{2,1,0:T(8,128)(2,1)S(1)}, bf16[16,40,256]{2,1,0:T(8,128)(2,1)S(1)}, u32[]{:S(2)}, u32[]{:S(2)}) collective-permute-start(bf16[16,40,256]{2,1,0:T(8,128)(2,1)S(1)} %all_to_all.5.refs_2_), channel_id=1, source_target_pairs={{0,2},{1,3},{2,0},{3,1},{4,6},{5,7},{6,4},{7,5},{8,10},{9,11},{10,... | collective-permute-start | bytes 983048 | tf_op jit(solution)/shard_map/ppermute | solution.py:456
  37.8 1.1 %turn_queries.1 = (bf16[1280,256]{1,0:T(8,128)(2,1)S(1)}, bf16[1280,256]{1,0:T(8,128)(2,1)S(1)}, f32[8,640]{1,0:T(8,128)S(1)}) custom-call(bf16[64,2560]{1,0:T(8,128)(2,1)S(1)} %copy-done.1, bf16[256,2560]{1,0:T(8,128)(2,1)S(1)} %copy-done, s32[16,128]{1,0:T(8,128)S(1)} %get-tuple-element.45.frames_ref, s32[16,128]{1,0:T(8,128)S(1)} %get-tuple-element.46.blocks_ref), custom_call_target="tpu_custom_call" | custom-call | flops 83886080 | bytes 3145728 | tf_op jit(solution)/shard_map/turn_queries/pallas_call | solution.py:315
  38.9 0.0 collective-permute-done.4.refs_3_
  38.9 3.6 %attend.4 = (f32[1280,128]{1,0:T(8,128)S(1)}, f32[1280,128]{1,0:T(8,128)S(1)}, f32[1280,256]{1,0:T(8,128)S(1)}) custom-call(bf16[1280,256]{1,0:T(8,128)(2,1)S(1)} %get-tuple-element.48.refs_0_, bf16[1280,256]{1,0:T(8,128)(2,1)S(1)} %get-tuple-element.49.refs_1_, bf16[16,40,256]{2,1,0:T(8,128)(2,1)S(1)} %all_to_all.5.refs_2_, ...), custom_call_target="tpu_custom_call" | custom-call | flops 2516582400 | bytes 6291456 | tf_op jit(solution)/shard_map/attend/pallas_call | solution.py:427
  42.5 2.8 %collective-permute-done.3.refs_3_ = bf16[16,40,256]{2,1,0:T(8,128)(2,1)S(1)} collective-permute-done((bf16[16,40,256]{2,1,0:T(8,128)(2,1)S(1)}, bf16[16,40,256]{2,1,0:T(8,128)(2,1)S(1)}, u32[]{:S(2)}, u32[]{:S(2)}) %collective-permute-start.3) | collective-permute-done | bytes 327712 | tf_op jit(solution)/shard_map/ppermute | solution.py:456
  45.2 0.7 %collective-permute-done.2.refs_2_ = bf16[16,40,256]{2,1,0:T(8,128)(2,1)S(1)} collective-permute-done((bf16[16,40,256]{2,1,0:T(8,128)(2,1)S(1)}, bf16[16,40,256]{2,1,0:T(8,128)(2,1)S(1)}, u32[]{:S(2)}, u32[]{:S(2)}) %collective-permute-start.2) | collective-permute-done | bytes 327712 | tf_op jit(solution)/shard_map/ppermute | solution.py:456
  46.0 0.8 %collective-permute-start.5 = (bf16[16,40,256]{2,1,0:T(8,128)(2,1)S(1)}, bf16[16,40,256]{2,1,0:T(8,128)(2,1)S(1)}, u32[]{:S(2)}, u32[]{:S(2)}) collective-permute-start(bf16[16,40,256]{2,1,0:T(8,128)(2,1)S(1)} %broadcast_select_fusion), channel_id=1, source_target_pairs={{0,6},{1,3},{2,4},{3,1},{4,2},{5,7},{6,0},{7,5},{8,14},{9,11},{10,... | collective-permute-start | bytes 983048 | tf_op jit(solution)/shard_map/ppermute | solution.py:456
  46.8 1.9 %collective-permute-start.7 = (bf16[16,40,256]{2,1,0:T(8,128)(2,1)S(1)}, bf16[16,40,256]{2,1,0:T(8,128)(2,1)S(1)}, u32[]{:S(2)}, u32[]{:S(2)}) collective-permute-start(bf16[16,40,256]{2,1,0:T(8,128)(2,1)S(1)} %collective-permute-done.2.refs_2_), channel_id=1, source_target_pairs={{0,1},{1,0},{2,3},{3,2},{4,5},{5,4},{6,7},{7,6},{8,9},{9,8},{10,11... | collective-permute-start | bytes 983048 | tf_op jit(solution)/shard_map/ppermute | solution.py:447
  48.7 4.1 %attend.5 = (f32[1280,128]{1,0:T(8,128)S(1)}, f32[1280,128]{1,0:T(8,128)S(1)}, f32[1280,256]{1,0:T(8,128)S(1)}) custom-call(bf16[1280,256]{1,0:T(8,128)(2,1)S(1)} %get-tuple-element.48.refs_0_, bf16[1280,256]{1,0:T(8,128)(2,1)S(1)} %get-tuple-element.49.refs_1_, ...), custom_call_target="tpu_custom_call", output_to_operand_aliasing={{0}: (5, {}), {1}: (6, {}), {2}: (7, {})} | custom-call | flops 2516582400 | bytes 6291456 | tf_op jit(solution)/shard_map/attend/pallas_call | solution.py:427
  52.8 0.0 copy-start.2
  52.8 2.7 %collective-permute-start.6 = (bf16[16,40,256]{2,1,0:T(8,128)(2,1)S(1)}, bf16[16,40,256]{2,1,0:T(8,128)(2,1)S(1)}, u32[]{:S(2)}, u32[]{:S(2)}) collective-permute-start(bf16[16,40,256]{2,1,0:T(8,128)(2,1)S(1)} %collective-permute-done.5.refs_2_), channel_id=1, source_target_pairs={{0,1},{1,0},{2,3},{3,2},{4,5},{5,4},{6,7},{7,6},{8,9},{9,8},{10,11... | collective-permute-start | bytes 983048 | tf_op jit(solution)/shard_map/ppermute | solution.py:447
  55.5 4.2 %attend.6 = (f32[1280,128]{1,0:T(8,128)S(1)}, f32[1280,128]{1,0:T(8,128)S(1)}, f32[1280,256]{1,0:T(8,128)S(1)}) custom-call(bf16[1280,256]{1,0:T(8,128)(2,1)S(1)} %get-tuple-element.48.refs_0_, bf16[1280,256]{1,0:T(8,128)(2,1)S(1)} %get-tuple-element.49.refs_1_, ...), custom_call_target="tpu_custom_call", output_to_operand_aliasing={{0}: (5, {}), {1}: (6, {}), {2}: (7, {})} | custom-call | flops 2516582400 | bytes 6291456 | tf_op jit(solution)/shard_map/attend/pallas_call | solution.py:427
  59.7 5.4 %attend.7 = bf16[64,2560]{1,0:T(8,128)(2,1)} custom-call(bf16[1280,256]{1,0:T(8,128)(2,1)S(1)} %get-tuple-element.48.refs_0_, bf16[1280,256]{1,0:T(8,128)(2,1)S(1)} %get-tuple-element.49.refs_1_, bf16[16,40,256]{2,1,0:T(8,128)(2,1)S(1)} %collective-permute-done.5.refs_2_, bf16[16,40,256]{2,1,0:T(8,128)(2,1)S(1)} %collective-permute-done.6.refs_3_, ...), custom_call_target="tpu_custom_call" | custom-call | flops 2516582400 | bytes 6291456 | tf_op jit(solution)/shard_map/attend/pallas_call | solution.py:427
  (10 shorter events, 0.1 us)
Async XLA Ops:
  1.7 11.2 %collective-permute-start.1 = (bf16[2,160,256]{2,1,0:T(8,128)(2,1)S(1)}, bf16[2,160,256]{2,1,0:T(8,128)(2,1)S(1)}, u32[]{:S(2)}, u32[]{:S(2)}) collective-permute-start(bf16[2,160,256]{2,1,0:T(8,128)(2,1)S(1)} %get-tuple-element.70), channel_id=1, source_target_pairs={{1,2},{2,1},{3,4},{4,3},{5,6},{6,5},{9,10},{10,9},{11,12},{12,11},... | collective-permute-start | bytes 491528 | tf_op jit(solution)/shard_map/ppermute | solution.py:469
  6.6 6.3 %collective-permute-start = (bf16[2,160,256]{2,1,0:T(8,128)(2,1)S(1)}, bf16[2,160,256]{2,1,0:T(8,128)(2,1)S(1)}, u32[]{:S(2)}, u32[]{:S(2)}) collective-permute-start(bf16[2,160,256]{2,1,0:T(8,128)(2,1)S(1)} %get-tuple-element.71), channel_id=1, source_target_pairs={{0,1},{1,0},{2,3},{3,2},{4,5},{5,4},{6,7},{7,6},{8,9},{9,8},{10,11... | collective-permute-start | bytes 491528 | tf_op jit(solution)/shard_map/ppermute | solution.py:447
  12.9 24.8 %copy-start = (bf16[256,2560]{1,0:T(8,128)(2,1)S(1)}, bf16[256,2560]{1,0:T(8,128)(2,1)}, u32[]{:S(2)}) copy-start(bf16[256,2560]{1,0:T(8,128)(2,1)} %wk_ref.1) | copy-start | bytes 3932164
  12.9 24.8 %copy-start.1 = (bf16[64,2560]{1,0:T(8,128)(2,1)S(1)}, bf16[64,2560]{1,0:T(8,128)(2,1)}, u32[]{:S(2)}) copy-start(bf16[64,2560]{1,0:T(8,128)(2,1)} %q_ref.1) | copy-start | bytes 983044
  32.5 6.4 %collective-permute-start.4 = (bf16[16,40,256]{2,1,0:T(8,128)(2,1)S(1)}, bf16[16,40,256]{2,1,0:T(8,128)(2,1)S(1)}, u32[]{:S(2)}, u32[]{:S(2)}) collective-permute-start(bf16[16,40,256]{2,1,0:T(8,128)(2,1)S(1)} %all_to_all.5.refs_2_), channel_id=1, source_target_pairs={{0,1},{1,0},{2,3},{3,2},{4,5},{5,4},{6,7},{7,6},{8,9},{9,8},{10,11... | collective-permute-start | bytes 983048 | tf_op jit(solution)/shard_map/ppermute | solution.py:447
  34.8 10.5 %collective-permute-start.3 = (bf16[16,40,256]{2,1,0:T(8,128)(2,1)S(1)}, bf16[16,40,256]{2,1,0:T(8,128)(2,1)S(1)}, u32[]{:S(2)}, u32[]{:S(2)}) collective-permute-start(bf16[16,40,256]{2,1,0:T(8,128)(2,1)S(1)} %all_to_all.5.refs_2_), channel_id=1, source_target_pairs={{0,6},{1,7},{2,4},{3,5},{4,2},{5,3},{6,0},{7,1},{8,14},{9,15},{10,... | collective-permute-start | bytes 983048 | tf_op jit(solution)/shard_map/ppermute | solution.py:456
  37.0 9.0 %collective-permute-start.2 = (bf16[16,40,256]{2,1,0:T(8,128)(2,1)S(1)}, bf16[16,40,256]{2,1,0:T(8,128)(2,1)S(1)}, u32[]{:S(2)}, u32[]{:S(2)}) collective-permute-start(bf16[16,40,256]{2,1,0:T(8,128)(2,1)S(1)} %all_to_all.5.refs_2_), channel_id=1, source_target_pairs={{0,2},{1,3},{2,0},{3,1},{4,6},{5,7},{6,4},{7,5},{8,10},{9,11},{10,... | collective-permute-start | bytes 983048 | tf_op jit(solution)/shard_map/ppermute | solution.py:456
  46.0 6.8 %collective-permute-start.5 = (bf16[16,40,256]{2,1,0:T(8,128)(2,1)S(1)}, bf16[16,40,256]{2,1,0:T(8,128)(2,1)S(1)}, u32[]{:S(2)}, u32[]{:S(2)}) collective-permute-start(bf16[16,40,256]{2,1,0:T(8,128)(2,1)S(1)} %broadcast_select_fusion), channel_id=1, source_target_pairs={{0,6},{1,3},{2,4},{3,1},{4,2},{5,7},{6,0},{7,5},{8,14},{9,11},{10,... | collective-permute-start | bytes 983048 | tf_op jit(solution)/shard_map/ppermute | solution.py:456
  46.8 8.7 %collective-permute-start.7 = (bf16[16,40,256]{2,1,0:T(8,128)(2,1)S(1)}, bf16[16,40,256]{2,1,0:T(8,128)(2,1)S(1)}, u32[]{:S(2)}, u32[]{:S(2)}) collective-permute-start(bf16[16,40,256]{2,1,0:T(8,128)(2,1)S(1)} %collective-permute-done.2.refs_2_), channel_id=1, source_target_pairs={{0,1},{1,0},{2,3},{3,2},{4,5},{5,4},{6,7},{7,6},{8,9},{9,8},{10,11... | collective-permute-start | bytes 983048 | tf_op jit(solution)/shard_map/ppermute | solution.py:447
  48.7 6.8 %collective-permute-start.8 = (bf16[16,40,256]{2,1,0:T(8,128)(2,1)S(1)}, bf16[16,40,256]{2,1,0:T(8,128)(2,1)S(1)}, u32[]{:S(2)}, u32[]{:S(2)}) collective-permute-start(bf16[16,40,256]{2,1,0:T(8,128)(2,1)S(1)} %collective-permute-done.3.refs_3_), channel_id=1, source_target_pairs={{0,1},{1,0},{2,3},{3,2},{4,5},{5,4},{6,7},{7,6},{8,9},{9,8},{10,11... | collective-permute-start | bytes 983048 | tf_op jit(solution)/shard_map/ppermute | solution.py:447
  52.8 6.9 %copy-start.2 = (bf16[256,2560]{1,0:T(8,128)(2,1)S(1)}, bf16[256,2560]{1,0:T(8,128)(2,1)}, u32[]{:S(2)}) copy-start(bf16[256,2560]{1,0:T(8,128)(2,1)} %refs_8_.1) | copy-start | bytes 3932164
  52.8 6.9 %collective-permute-start.6 = (bf16[16,40,256]{2,1,0:T(8,128)(2,1)S(1)}, bf16[16,40,256]{2,1,0:T(8,128)(2,1)S(1)}, u32[]{:S(2)}, u32[]{:S(2)}) collective-permute-start(bf16[16,40,256]{2,1,0:T(8,128)(2,1)S(1)} %collective-permute-done.5.refs_2_), channel_id=1, source_target_pairs={{0,1},{1,0},{2,3},{3,2},{4,5},{5,4},{6,7},{7,6},{8,9},{9,8},{10,11... | collective-permute-start | bytes 983048 | tf_op jit(solution)/shard_map/ppermute | solution.py:447

commit v3 on v2

--- a/solution.py
+++ b/solution.py
@@ -77,12 +77,10 @@
     copies = [
         pltpu.make_async_copy(src, dst, sems.at[k]) for k, (src, dst) in enumerate(pairs)
     ]
-    for copy in copies:
-        copy.start()
+    for k in (2, 0, 3, 4, 5, 1, 6):
+        copies[k].start()
     copies[0].wait()
-    copies[1].wait()
     g1 = g1_ref[...] * 0.5
-    g2 = g2_ref[...] * 0.5
 
     def first_rows(rows):
         for row in rows:
@@ -94,7 +92,7 @@
             [first_ref[start + step : start + step + count] for step in range(3)], w1_ref
         )
 
-    def second_rows(rows, total):
+    def second_rows(rows, total, g2):
         for k, row in enumerate(rows):
             middle = x_ref[row + 1].astype(jnp.float32) + total[k * W : (k + 1) * W]
             middle_ref[row] = middle.astype(jnp.bfloat16)
@@ -102,22 +100,28 @@
 
     copies[2].wait()
     first_rows(range(0, chunk))
-    for copy in copies[3:]:
-        copy.wait()
+    for k in (3, 4, 5, 1, 6):
+        copies[k].wait()
+    later = copies[7:]
+    for copy in later:
+        copy.start()
+    g2 = g2_ref[...] * 0.5
     first_rows(range(chunk, 7))
     parts = [range(0, 5), range(5, 10), range(10, INNER)]
     totals = [middle_rows(parts[0])]
     first_rows(range(7, 12))
     totals.append(middle_rows(parts[1]))
     first_rows(range(12, ROWS))
-    second_rows(parts[0], totals[0])
+    second_rows(parts[0], totals[0], g2)
     totals.append(middle_rows(parts[2]))
     for k in range(2):
         sides_ref[k] = first_ref[k]
         sides_ref[2 + k] = first_ref[ROWS - 2 + k]
         base_ref[k] = x_ref[k * (ROWS - 1)]
-    second_rows(parts[1], totals[1])
-    second_rows(parts[2], totals[2])
+    second_rows(parts[1], totals[1], g2)
+    second_rows(parts[2], totals[2], g2)
+    for copy in later:
+        copy.wait()
 
 
 def inner_call(latents, w1, w2, g1, g2, gk, frame_ids, block_ids):
@@ -207,6 +211,7 @@
         w1_ref,
     )
     second_rows(total, range(2, 2 + half))
+    copies = [send(0, 2, half)]
     total = dot_rows([inner_ref[half + step : 2 * half + step] for step in range(3)], w2_ref)
 
     bases = [low[1], base_ref[0].astype(jnp.float32), base_ref[1].astype(jnp.float32), high[0]]
@@ -228,15 +233,17 @@
         w2_ref,
     )
     second_rows(total, range(2 + half, ROWS - 2))
+    copies.append(send(1, 2 + half, half))
     second_rows(edges, [0, 1, ROWS - 2, ROWS - 1])
-    copy = send(0, 0, ROWS)
+    copies += [send(2, 0, 2), send(3, ROWS - 2, 2)]
 
     gk = gk_ref[...]
     for g in range(FRAMES):
         at = pl.multiple_of(picks[g] * BT, 8)
         block = normalized(wide_ref[pl.ds(at, BT)], gk)
         picked_ref[g] = block.astype(jnp.bfloat16)
-    copy.wait()
+    for copy in copies:
+        copy.wait()
 
 
 def outer_call(near, away, inner):
@@ -255,7 +262,7 @@
             pltpu.VMEM((4, W, C), jnp.bfloat16),
             pltpu.VMEM((8, W, 3 * C), jnp.bfloat16),
             pltpu.VMEM((ROWS * W, C), jnp.float32),
-            pltpu.SemaphoreType.DMA((1,)),
+            pltpu.SemaphoreType.DMA((4,)),
         ],
         compiler_params=pltpu.CompilerParams(vmem_limit_bytes=28 * 1024 * 1024),
         cost_estimate=pl.CostEstimate(
@@ -325,7 +332,7 @@
     )(queries, key_weight, frame_ids, block_ids)
 
 
-BLOCK = 320
+BLOCK = 256
 SLAB = 32
 
 
@@ -436,7 +443,7 @@
             pltpu.VMEM((2, BLOCK, tokens), jnp.float32),
             pltpu.VMEM((2, BLOCK, tokens), jnp.bfloat16),
         ],
-        compiler_params=pltpu.CompilerParams(vmem_limit_bytes=40 * 1024 * 1024),
+        compiler_params=pltpu.CompilerParams(vmem_limit_bytes=24 * 1024 * 1024),
         cost_estimate=pl.CostEstimate(
             flops=6 * QROWS * C * tokens, bytes_accessed=6 << 20, transcendentals=QROWS * tokens
         ),
@@ -487,9 +494,9 @@
     even_swap = core_swap(even_side)
     odd_swap = core_swap(odd_side)
     state = attend_call(qh, ql, (even_side, odd_side), bias, 1, state)
+    state = attend_call(qh, ql, (even_swap, odd_swap), bias, 2, state)
     far, state = lax.optimization_barrier((far, state))
     far_swap = core_swap(far)
-    state = attend_call(qh, ql, (even_swap, odd_swap), bias, 2, state)
     attended = attend_call(qh, ql, (far, far_swap), bias, 3, state, value_weight)
     return (refined[None], attended)
 

time: 65.3 us -> 63.6 us (0.974)
  starting transfers between devices: 15.7 us -> 13.6 us
  waiting for transfers between devices: 3.51 us -> 4.88 us
  Pallas kernels: 29.7 us -> 28.7 us
    ppermute x5, starting transfers between devices: 6.94 us -> 4.82 us  [core_swap(): return lax.ppermute(x, 'tile', [(t, t ^ 1) for t in range(TILES)])]
    ppermute x5, waiting for transfers between devices: 0.01 us -> 1.27 us  [core_swap(): return lax.ppermute(x, 'tile', [(t, t ^ 1) for t in range(TILES)])]
  transfers between devices with their start and end apart: 9 -> 9, of which waited for: 2 -> 3; matrix products, arithmetic and copies ran while one was open for 0% -> 0% of each run, Pallas kernels for 29% -> 29%
where the time goes in v3:
time: 63.6 us; the launch traced here: 63.4 us
  Pallas kernels  28.7 us (45%)
  blocking collectives  14.4 us (23%)
  starting transfers between devices  13.6 us (21%)
  waiting for transfers between devices  4.88 us (8%)
  local copies, waits for them, and re-layouts  1.04 us (2%)
  between operations  0.79 us (1%)
    pallas_call x4, Pallas kernels, attend_call(): pl.pallas_call(functools.partial(attend_kernel, first, last, len(parts),...  16.7 us
    all_to_all x1, blocking collectives, local(): lax.all_to_all(picked, 'frames', split_axis=0, concat_axis=0, tiled=True)  14.4 us
    pallas_call x1, Pallas kernels, inner_call(): pl.pallas_call(inner_kernel, name='inner_rows', out_shape=out_shape, in_s...  5.85 us
    pallas_call x1, Pallas kernels, outer_call(): pl.pallas_call(outer_kernel, name='outer_rows', out_shape=(jax.ShapeDtype...  4.99 us
    ppermute x1, starting transfers between devices, local(): away = lax.ppermute(away, 'tile', across)  4.92 us
    ppermute x5, starting transfers between devices, core_swap(): return lax.ppermute(x, 'tile', [(t, t ^ 1) for t in range(TILES)])  4.82 us
    ppermute x3, starting transfers between devices, plane_swap(): return lax.ppermute(x, 'tile', pairs)  3.83 us
    ppermute x3, waiting for transfers between devices, plane_swap(): return lax.ppermute(x, 'tile', pairs)  3.61 us
  transfers between devices with their start and end apart: 9, of which 3 were waited for; matrix products, arithmetic and copies ran while one was open for 0% of the time, Pallas kernels for 29%

profile of v3, /device:TPU:1, one launch (start us, length us, event | category | flops | bytes accessed | tf_op | source)
XLA Modules:
  0.0 63.4 jit_solution(12496000336154333263)
XLA Ops:
  0.6 1.0 %dynamic-slice_bitcast_fusion = (bf16[2,160,256]{2,1,0:T(8,128)(2,1)S(1)}, bf16[2,160,256]{2,1,0:T(8,128)(2,1)S(1)}) fusion(bf16[1,16,160,256]{3,2,1,0:T(8,128)(2,1)} %param.12, s32[]{:T(128)S(6)} %select_n.15, s32[]{:T(128)S(6)} %select_n.14), kind=kLoop, calls=%fused_computation.1 | loop fusion | bytes 655368 | tf_op jit(solution)/shard_map/dynamic_slice | solution.py:473
  1.7 4.9 %collective-permute-start.1 = (bf16[2,160,256]{2,1,0:T(8,128)(2,1)S(1)}, bf16[2,160,256]{2,1,0:T(8,128)(2,1)S(1)}, u32[]{:S(2)}, u32[]{:S(2)}) collective-permute-start(bf16[2,160,256]{2,1,0:T(8,128)(2,1)S(1)} %get-tuple-element.70), channel_id=1, source_target_pairs={{1,2},{2,1},{3,4},{4,3},{5,6},{6,5},{9,10},{10,9},{11,12},{12,11},... | collective-permute-start | bytes 491528 | tf_op jit(solution)/shard_map/ppermute | solution.py:476
  6.6 0.1 collective-permute-start
  6.7 5.9 %inner_rows.1 = (bf16[14,160,768]{2,1,0:T(8,128)(2,1)S(1)}, bf16[14,160,256]{2,1,0:T(8,128)(2,1)S(1)}, bf16[4,160,768]{2,1,0:T(8,128)(2,1)S(1)}, bf16[2,160,256]...) custom-call(bf16[16,160,256]{2,1,0:T(8,128)(2,1)} %bitcast.11, ...), custom_call_target="tpu_custom_call" | custom-call | flops 2642411520 | bytes 4194304 | tf_op jit(solution)/shard_map/inner_rows/pallas_call | solution.py:138
  12.6 0.0 copy-start
  12.6 0.0 copy-start.1
  12.6 5.0 %outer_rows.1 = (bf16[16,160,256]{2,1,0:T(8,128)(2,1)}, bf16[16,40,256]{2,1,0:T(8,128)(2,1)S(1)}) custom-call(bf16[2,160,256]{2,1,0:T(8,128)(2,1)S(1)} %collective-permute-done.near_ref, bf16[2,160,256]{2,1,0:T(8,128)(2,1)S(1)} %collective-permute-done.1.away_ref, bf16[14,160,768]{2,1,0:T(8,128)(2,1)S(1)} %get-tuple-element.36.inner_ref, ...), custom_call_target="tpu_custom_call" | custom-call | flops 3774873600 | bytes 4194304 | tf_op jit(solution)/shard_map/outer_rows/pallas_call | solution.py:250
  17.6 14.4 %all_to_all.5.refs_2_ = bf16[16,40,256]{2,1,0:T(8,128)(2,1)S(1)} all-to-all(bf16[16,40,256]{2,1,0:T(8,128)(2,1)S(1)} %get-tuple-element.50), channel_id=1, replica_groups=mesh['frames'=16,'tile'=8] {'frames'}, dimensions={0} | all-to-all | bytes 655360 | tf_op jit(solution)/shard_map/all_to_all | solution.py:487
  32.0 2.3 %collective-permute-start.4 = (bf16[16,40,256]{2,1,0:T(8,128)(2,1)S(1)}, bf16[16,40,256]{2,1,0:T(8,128)(2,1)S(1)}, u32[]{:S(2)}, u32[]{:S(2)}) collective-permute-start(bf16[16,40,256]{2,1,0:T(8,128)(2,1)S(1)} %all_to_all.5.refs_2_), channel_id=1, source_target_pairs={{0,1},{1,0},{2,3},{3,2},{4,5},{5,4},{6,7},{7,6},{8,9},{9,8},{10,11... | collective-permute-start | bytes 983048 | tf_op jit(solution)/shard_map/ppermute | solution.py:454
  34.3 2.2 %collective-permute-start.3 = (bf16[16,40,256]{2,1,0:T(8,128)(2,1)S(1)}, bf16[16,40,256]{2,1,0:T(8,128)(2,1)S(1)}, u32[]{:S(2)}, u32[]{:S(2)}) collective-permute-start(bf16[16,40,256]{2,1,0:T(8,128)(2,1)S(1)} %all_to_all.5.refs_2_), channel_id=1, source_target_pairs={{0,6},{1,7},{2,4},{3,5},{4,2},{5,3},{6,0},{7,1},{8,14},{9,15},{10,... | collective-permute-start | bytes 983048 | tf_op jit(solution)/shard_map/ppermute | solution.py:463
  36.5 0.8 %collective-permute-start.2 = (bf16[16,40,256]{2,1,0:T(8,128)(2,1)S(1)}, bf16[16,40,256]{2,1,0:T(8,128)(2,1)S(1)}, u32[]{:S(2)}, u32[]{:S(2)}) collective-permute-start(bf16[16,40,256]{2,1,0:T(8,128)(2,1)S(1)} %all_to_all.5.refs_2_), channel_id=1, source_target_pairs={{0,2},{1,3},{2,0},{3,1},{4,6},{5,7},{6,4},{7,5},{8,10},{9,11},{10,... | collective-permute-start | bytes 983048 | tf_op jit(solution)/shard_map/ppermute | solution.py:463
  37.3 1.1 %turn_queries.1 = (bf16[1280,256]{1,0:T(8,128)(2,1)S(1)}, bf16[1280,256]{1,0:T(8,128)(2,1)S(1)}, f32[8,640]{1,0:T(8,128)S(1)}) custom-call(bf16[64,2560]{1,0:T(8,128)(2,1)S(1)} %copy-done.1, bf16[256,2560]{1,0:T(8,128)(2,1)S(1)} %copy-done, s32[16,128]{1,0:T(8,128)S(1)} %get-tuple-element.45.frames_ref, s32[16,128]{1,0:T(8,128)S(1)} %get-tuple-element.46.blocks_ref), custom_call_target="tpu_custom_call" | custom-call | flops 83886080 | bytes 3145728 | tf_op jit(solution)/shard_map/turn_queries/pallas_call | solution.py:322
  38.4 3.4 %attend.4 = (f32[1280,128]{1,0:T(8,128)S(1)}, f32[1280,128]{1,0:T(8,128)S(1)}, f32[1280,256]{1,0:T(8,128)S(1)}) custom-call(bf16[1280,256]{1,0:T(8,128)(2,1)S(1)} %get-tuple-element.48.refs_0_, bf16[1280,256]{1,0:T(8,128)(2,1)S(1)} %get-tuple-element.49.refs_1_, bf16[16,40,256]{2,1,0:T(8,128)(2,1)S(1)} %all_to_all.5.refs_2_, ...), custom_call_target="tpu_custom_call" | custom-call | flops 2516582400 | bytes 6291456 | tf_op jit(solution)/shard_map/attend/pallas_call | solution.py:434
  41.9 2.9 %collective-permute-done.3.refs_3_ = bf16[16,40,256]{2,1,0:T(8,128)(2,1)S(1)} collective-permute-done((bf16[16,40,256]{2,1,0:T(8,128)(2,1)S(1)}, bf16[16,40,256]{2,1,0:T(8,128)(2,1)S(1)}, u32[]{:S(2)}, u32[]{:S(2)}) %collective-permute-start.3) | collective-permute-done | bytes 327712 | tf_op jit(solution)/shard_map/ppermute | solution.py:463
  44.7 0.7 %collective-permute-done.2.refs_2_ = bf16[16,40,256]{2,1,0:T(8,128)(2,1)S(1)} collective-permute-done((bf16[16,40,256]{2,1,0:T(8,128)(2,1)S(1)}, bf16[16,40,256]{2,1,0:T(8,128)(2,1)S(1)}, u32[]{:S(2)}, u32[]{:S(2)}) %collective-permute-start.2) | collective-permute-done | bytes 327712 | tf_op jit(solution)/shard_map/ppermute | solution.py:463
  45.5 1.1 %collective-permute-start.6 = (bf16[16,40,256]{2,1,0:T(8,128)(2,1)S(1)}, bf16[16,40,256]{2,1,0:T(8,128)(2,1)S(1)}, u32[]{:S(2)}, u32[]{:S(2)}) collective-permute-start(bf16[16,40,256]{2,1,0:T(8,128)(2,1)S(1)} %collective-permute-done.2.refs_2_), channel_id=1, source_target_pairs={{0,1},{1,0},{2,3},{3,2},{4,5},{5,4},{6,7},{7,6},{8,9},{9,8},{10,11... | collective-permute-start | bytes 983048 | tf_op jit(solution)/shard_map/ppermute | solution.py:454
  46.6 0.0 collective-permute-start.7
  46.7 0.8 %collective-permute-start.5 = (bf16[16,40,256]{2,1,0:T(8,128)(2,1)S(1)}, bf16[16,40,256]{2,1,0:T(8,128)(2,1)S(1)}, u32[]{:S(2)}, u32[]{:S(2)}) collective-permute-start(bf16[16,40,256]{2,1,0:T(8,128)(2,1)S(1)} %broadcast_select_fusion), channel_id=1, source_target_pairs={{0,6},{1,3},{2,4},{3,1},{4,2},{5,7},{6,0},{7,5},{8,14},{9,11},{10,... | collective-permute-start | bytes 983048 | tf_op jit(solution)/shard_map/ppermute | solution.py:463
  47.5 3.9 %attend.5 = (f32[1280,128]{1,0:T(8,128)S(1)}, f32[1280,128]{1,0:T(8,128)S(1)}, f32[1280,256]{1,0:T(8,128)S(1)}) custom-call(bf16[1280,256]{1,0:T(8,128)(2,1)S(1)} %get-tuple-element.48.refs_0_, bf16[1280,256]{1,0:T(8,128)(2,1)S(1)} %get-tuple-element.49.refs_1_, ...), custom_call_target="tpu_custom_call", output_to_operand_aliasing={{0}: (5, {}), {1}: (6, {}), {2}: (7, {})} | custom-call | flops 2516582400 | bytes 6291456 | tf_op jit(solution)/shard_map/attend/pallas_call | solution.py:434
  51.5 0.0 copy-start.2
  51.5 4.0 %attend.6 = (f32[1280,128]{1,0:T(8,128)S(1)}, f32[1280,128]{1,0:T(8,128)S(1)}, f32[1280,256]{1,0:T(8,128)S(1)}) custom-call(bf16[1280,256]{1,0:T(8,128)(2,1)S(1)} %get-tuple-element.48.refs_0_, bf16[1280,256]{1,0:T(8,128)(2,1)S(1)} %get-tuple-element.49.refs_1_, ...), custom_call_target="tpu_custom_call", output_to_operand_aliasing={{0}: (5, {}), {1}: (6, {}), {2}: (7, {})} | custom-call | flops 2516582400 | bytes 6291456 | tf_op jit(solution)/shard_map/attend/pallas_call | solution.py:434
  55.5 1.3 %collective-permute-start.8 = (bf16[16,40,256]{2,1,0:T(8,128)(2,1)S(1)}, bf16[16,40,256]{2,1,0:T(8,128)(2,1)S(1)}, u32[]{:S(2)}, u32[]{:S(2)}) collective-permute-start(bf16[16,40,256]{2,1,0:T(8,128)(2,1)S(1)} %collective-permute-done.5.refs_2_), channel_id=1, source_target_pairs={{0,1},{1,0},{2,3},{3,2},{4,5},{5,4},{6,7},{7,6},{8,9},{9,8},{10,11... | collective-permute-start | bytes 983048 | tf_op jit(solution)/shard_map/ppermute | solution.py:454
  56.8 1.3 %collective-permute-done.8.refs_3_ = bf16[16,40,256]{2,1,0:T(8,128)(2,1)S(1)} collective-permute-done((bf16[16,40,256]{2,1,0:T(8,128)(2,1)S(1)}, bf16[16,40,256]{2,1,0:T(8,128)(2,1)S(1)}, u32[]{:S(2)}, u32[]{:S(2)}) %collective-permute-start.8) | collective-permute-done | bytes 327712 | tf_op jit(solution)/shard_map/ppermute | solution.py:454
  58.1 5.3 %attend.7 = bf16[64,2560]{1,0:T(8,128)(2,1)} custom-call(bf16[1280,256]{1,0:T(8,128)(2,1)S(1)} %get-tuple-element.48.refs_0_, bf16[1280,256]{1,0:T(8,128)(2,1)S(1)} %get-tuple-element.49.refs_1_, bf16[16,40,256]{2,1,0:T(8,128)(2,1)S(1)} %collective-permute-done.5.refs_2_, bf16[16,40,256]{2,1,0:T(8,128)(2,1)S(1)} %collective-permute-done.8.refs_3_, ...), custom_call_target="tpu_custom_call" | custom-call | flops 2516582400 | bytes 6291456 | tf_op jit(solution)/shard_map/attend/pallas_call | solution.py:434
  (10 shorter events, 0.1 us)
Async XLA Ops:
  1.7 10.9 %collective-permute-start.1 = (bf16[2,160,256]{2,1,0:T(8,128)(2,1)S(1)}, bf16[2,160,256]{2,1,0:T(8,128)(2,1)S(1)}, u32[]{:S(2)}, u32[]{:S(2)}) collective-permute-start(bf16[2,160,256]{2,1,0:T(8,128)(2,1)S(1)} %get-tuple-element.70), channel_id=1, source_target_pairs={{1,2},{2,1},{3,4},{4,3},{5,6},{6,5},{9,10},{10,9},{11,12},{12,11},... | collective-permute-start | bytes 491528 | tf_op jit(solution)/shard_map/ppermute | solution.py:476
  6.6 6.0 %collective-permute-start = (bf16[2,160,256]{2,1,0:T(8,128)(2,1)S(1)}, bf16[2,160,256]{2,1,0:T(8,128)(2,1)S(1)}, u32[]{:S(2)}, u32[]{:S(2)}) collective-permute-start(bf16[2,160,256]{2,1,0:T(8,128)(2,1)S(1)} %get-tuple-element.71), channel_id=1, source_target_pairs={{0,1},{1,0},{2,3},{3,2},{4,5},{5,4},{6,7},{7,6},{8,9},{9,8},{10,11... | collective-permute-start | bytes 491528 | tf_op jit(solution)/shard_map/ppermute | solution.py:454
  12.6 24.7 %copy-start = (bf16[256,2560]{1,0:T(8,128)(2,1)S(1)}, bf16[256,2560]{1,0:T(8,128)(2,1)}, u32[]{:S(2)}) copy-start(bf16[256,2560]{1,0:T(8,128)(2,1)} %wk_ref.1) | copy-start | bytes 3932164
  12.6 24.7 %copy-start.1 = (bf16[64,2560]{1,0:T(8,128)(2,1)S(1)}, bf16[64,2560]{1,0:T(8,128)(2,1)}, u32[]{:S(2)}) copy-start(bf16[64,2560]{1,0:T(8,128)(2,1)} %q_ref.1) | copy-start | bytes 983044
  32.0 6.4 %collective-permute-start.4 = (bf16[16,40,256]{2,1,0:T(8,128)(2,1)S(1)}, bf16[16,40,256]{2,1,0:T(8,128)(2,1)S(1)}, u32[]{:S(2)}, u32[]{:S(2)}) collective-permute-start(bf16[16,40,256]{2,1,0:T(8,128)(2,1)S(1)} %all_to_all.5.refs_2_), channel_id=1, source_target_pairs={{0,1},{1,0},{2,3},{3,2},{4,5},{5,4},{6,7},{7,6},{8,9},{9,8},{10,11... | collective-permute-start | bytes 983048 | tf_op jit(solution)/shard_map/ppermute | solution.py:454
  34.3 10.5 %collective-permute-start.3 = (bf16[16,40,256]{2,1,0:T(8,128)(2,1)S(1)}, bf16[16,40,256]{2,1,0:T(8,128)(2,1)S(1)}, u32[]{:S(2)}, u32[]{:S(2)}) collective-permute-start(bf16[16,40,256]{2,1,0:T(8,128)(2,1)S(1)} %all_to_all.5.refs_2_), channel_id=1, source_target_pairs={{0,6},{1,7},{2,4},{3,5},{4,2},{5,3},{6,0},{7,1},{8,14},{9,15},{10,... | collective-permute-start | bytes 983048 | tf_op jit(solution)/shard_map/ppermute | solution.py:463
  36.5 9.0 %collective-permute-start.2 = (bf16[16,40,256]{2,1,0:T(8,128)(2,1)S(1)}, bf16[16,40,256]{2,1,0:T(8,128)(2,1)S(1)}, u32[]{:S(2)}, u32[]{:S(2)}) collective-permute-start(bf16[16,40,256]{2,1,0:T(8,128)(2,1)S(1)} %all_to_all.5.refs_2_), channel_id=1, source_target_pairs={{0,2},{1,3},{2,0},{3,1},{4,6},{5,7},{6,4},{7,5},{8,10},{9,11},{10,... | collective-permute-start | bytes 983048 | tf_op jit(solution)/shard_map/ppermute | solution.py:463
  45.5 6.0 %collective-permute-start.6 = (bf16[16,40,256]{2,1,0:T(8,128)(2,1)S(1)}, bf16[16,40,256]{2,1,0:T(8,128)(2,1)S(1)}, u32[]{:S(2)}, u32[]{:S(2)}) collective-permute-start(bf16[16,40,256]{2,1,0:T(8,128)(2,1)S(1)} %collective-permute-done.2.refs_2_), channel_id=1, source_target_pairs={{0,1},{1,0},{2,3},{3,2},{4,5},{5,4},{6,7},{7,6},{8,9},{9,8},{10,11... | collective-permute-start | bytes 983048 | tf_op jit(solution)/shard_map/ppermute | solution.py:454
  46.6 4.8 %collective-permute-start.7 = (bf16[16,40,256]{2,1,0:T(8,128)(2,1)S(1)}, bf16[16,40,256]{2,1,0:T(8,128)(2,1)S(1)}, u32[]{:S(2)}, u32[]{:S(2)}) collective-permute-start(bf16[16,40,256]{2,1,0:T(8,128)(2,1)S(1)} %collective-permute-done.3.refs_3_), channel_id=1, source_target_pairs={{0,1},{1,0},{2,3},{3,2},{4,5},{5,4},{6,7},{7,6},{8,9},{9,8},{10,11... | collective-permute-start | bytes 983048 | tf_op jit(solution)/shard_map/ppermute | solution.py:454
  46.7 8.8 %collective-permute-start.5 = (bf16[16,40,256]{2,1,0:T(8,128)(2,1)S(1)}, bf16[16,40,256]{2,1,0:T(8,128)(2,1)S(1)}, u32[]{:S(2)}, u32[]{:S(2)}) collective-permute-start(bf16[16,40,256]{2,1,0:T(8,128)(2,1)S(1)} %broadcast_select_fusion), channel_id=1, source_target_pairs={{0,6},{1,3},{2,4},{3,1},{4,2},{5,7},{6,0},{7,5},{8,14},{9,11},{10,... | collective-permute-start | bytes 983048 | tf_op jit(solution)/shard_map/ppermute | solution.py:463
  51.5 6.6 %copy-start.2 = (bf16[256,2560]{1,0:T(8,128)(2,1)S(1)}, bf16[256,2560]{1,0:T(8,128)(2,1)}, u32[]{:S(2)}) copy-start(bf16[256,2560]{1,0:T(8,128)(2,1)} %refs_8_.1) | copy-start | bytes 3932164
  55.5 2.6 %collective-permute-start.8 = (bf16[16,40,256]{2,1,0:T(8,128)(2,1)S(1)}, bf16[16,40,256]{2,1,0:T(8,128)(2,1)S(1)}, u32[]{:S(2)}, u32[]{:S(2)}) collective-permute-start(bf16[16,40,256]{2,1,0:T(8,128)(2,1)S(1)} %collective-permute-done.5.refs_2_), channel_id=1, source_target_pairs={{0,1},{1,0},{2,3},{3,2},{4,5},{5,4},{6,7},{7,6},{8,9},{9,8},{10,11... | collective-permute-start | bytes 983048 | tf_op jit(solution)/shard_map/ppermute | solution.py:454

commit v4 on v3

--- a/solution.py
+++ b/solution.py
@@ -374,26 +374,31 @@
         if block + 1 < blocks:
             scores(block + 1, 1 - slot)
         alphas = []
+        peaks = []
         sums = []
+        slabs = range(block * BLOCK, (block + 1) * BLOCK, SLAB)
+        if not first:
+            old_peaks = [m_in[at : at + SLAB, 0:1] for at in slabs]
+            old_sums = [l_in[at : at + SLAB, 0:1] for at in slabs]
         for slab in range(BLOCK // SLAB):
             own = slice(slab * SLAB, (slab + 1) * SLAB)
-            rows = slice(block * BLOCK + slab * SLAB, block * BLOCK + (slab + 1) * SLAB)
             s = s_ref[slot, own] + bias
             peak = jnp.max(s, axis=-1, keepdims=True)
             if not first:
-                old = m_in[rows, 0:1]
+                old = old_peaks[slab]
                 peak = jnp.maximum(peak, old)
                 alphas.append(jnp.exp2(old - peak))
             p = jnp.exp2(s - peak)
             total = jnp.sum(p, axis=-1, keepdims=True)
             if not first:
-                total = total + alphas[-1] * l_in[rows, 0:1]
+                total = total + alphas[-1] * old_sums[slab]
             p_ref[slot, own] = p.astype(jnp.bfloat16)
-            if last:
-                sums.append(total)
-            else:
-                m_out[rows] = jnp.broadcast_to(peak, (SLAB, 128))
-                l_out[rows] = jnp.broadcast_to(total, (SLAB, 128))
+            peaks.append(peak)
+            sums.append(total)
+        if not last:
+            for slab, at in enumerate(slabs):
+                m_out[at : at + SLAB] = jnp.broadcast_to(peaks[slab], (SLAB, 128))
+                l_out[at : at + SLAB] = jnp.broadcast_to(sums[slab], (SLAB, 128))
         rows = slice(block * BLOCK, (block + 1) * BLOCK)
         mixed = jnp.dot(p_ref[slot], x_ref[...], preferred_element_type=jnp.float32)
         if not first:
@@ -421,7 +426,7 @@
     aliases = {}
     if not first:
         if not last:
-            aliases = {len(operands) + k: k for k in range(3)}
+            aliases = {}
         operands += list(state)
     if last:
         operands.append(value_weight)

time: 63.6 us -> 63.4 us (level)
  transfers between devices with their start and end apart: 9 -> 9, of which waited for: 3 -> 3; matrix products, arithmetic and copies ran while one was open for 0% -> 0% of each run, Pallas kernels for 29% -> 28%
where the time goes in v4:
time: 63.4 us; the launch traced here: 63.1 us
  Pallas kernels  28.1 us (44%)
  blocking collectives  14.4 us (23%)
  starting transfers between devices  13.8 us (22%)
  waiting for transfers between devices  4.95 us (8%)
  local copies, waits for them, and re-layouts  1.04 us (2%)
  between operations  0.79 us (1%)
    pallas_call x4, Pallas kernels, attend_call(): pl.pallas_call(functools.partial(attend_kernel, first, last, len(parts),...  16.2 us
    all_to_all x1, blocking collectives, local(): lax.all_to_all(picked, 'frames', split_axis=0, concat_axis=0, tiled=True)  14.4 us
    pallas_call x1, Pallas kernels, inner_call(): pl.pallas_call(inner_kernel, name='inner_rows', out_shape=out_shape, in_s...  5.85 us
    ppermute x5, starting transfers between devices, core_swap(): return lax.ppermute(x, 'tile', [(t, t ^ 1) for t in range(TILES)])  5.05 us
    pallas_call x1, Pallas kernels, outer_call(): pl.pallas_call(outer_kernel, name='outer_rows', out_shape=(jax.ShapeDtype...  4.99 us
    ppermute x1, starting transfers between devices, local(): away = lax.ppermute(away, 'tile', across)  4.92 us
    ppermute x3, starting transfers between devices, plane_swap(): return lax.ppermute(x, 'tile', pairs)  3.83 us
    ppermute x3, waiting for transfers between devices, plane_swap(): return lax.ppermute(x, 'tile', pairs)  3.68 us
  transfers between devices with their start and end apart: 9, of which 3 were waited for; matrix products, arithmetic and copies ran while one was open for 0% of the time, Pallas kernels for 28%

profile of v4, /device:TPU:1, one launch (start us, length us, event | category | flops | bytes accessed | tf_op | source)
XLA Modules:
  0.0 63.1 jit_solution(16859470507154935595)
XLA Ops:
  0.6 1.0 %dynamic-slice_bitcast_fusion = (bf16[2,160,256]{2,1,0:T(8,128)(2,1)S(1)}, bf16[2,160,256]{2,1,0:T(8,128)(2,1)S(1)}) fusion(bf16[1,16,160,256]{3,2,1,0:T(8,128)(2,1)} %param.12, s32[]{:T(128)S(6)} %select_n.15, s32[]{:T(128)S(6)} %select_n.14), kind=kLoop, calls=%fused_computation.1 | loop fusion | bytes 655368 | tf_op jit(solution)/shard_map/dynamic_slice | solution.py:478
  1.7 4.9 %collective-permute-start.1 = (bf16[2,160,256]{2,1,0:T(8,128)(2,1)S(1)}, bf16[2,160,256]{2,1,0:T(8,128)(2,1)S(1)}, u32[]{:S(2)}, u32[]{:S(2)}) collective-permute-start(bf16[2,160,256]{2,1,0:T(8,128)(2,1)S(1)} %get-tuple-element.70), channel_id=1, source_target_pairs={{1,2},{2,1},{3,4},{4,3},{5,6},{6,5},{9,10},{10,9},{11,12},{12,11},... | collective-permute-start | bytes 491528 | tf_op jit(solution)/shard_map/ppermute | solution.py:481
  6.6 0.1 collective-permute-start
  6.7 5.9 %inner_rows.1 = (bf16[14,160,768]{2,1,0:T(8,128)(2,1)S(1)}, bf16[14,160,256]{2,1,0:T(8,128)(2,1)S(1)}, bf16[4,160,768]{2,1,0:T(8,128)(2,1)S(1)}, bf16[2,160,256]...) custom-call(bf16[16,160,256]{2,1,0:T(8,128)(2,1)} %bitcast.11, ...), custom_call_target="tpu_custom_call" | custom-call | flops 2642411520 | bytes 4194304 | tf_op jit(solution)/shard_map/inner_rows/pallas_call | solution.py:138
  12.6 0.0 copy-start
  12.6 0.0 copy-start.1
  12.6 5.0 %outer_rows.1 = (bf16[16,160,256]{2,1,0:T(8,128)(2,1)}, bf16[16,40,256]{2,1,0:T(8,128)(2,1)S(1)}) custom-call(bf16[2,160,256]{2,1,0:T(8,128)(2,1)S(1)} %collective-permute-done.near_ref, bf16[2,160,256]{2,1,0:T(8,128)(2,1)S(1)} %collective-permute-done.1.away_ref, bf16[14,160,768]{2,1,0:T(8,128)(2,1)S(1)} %get-tuple-element.36.inner_ref, ...), custom_call_target="tpu_custom_call" | custom-call | flops 3774873600 | bytes 4194304 | tf_op jit(solution)/shard_map/outer_rows/pallas_call | solution.py:250
  17.6 14.4 %all_to_all.5.refs_2_ = bf16[16,40,256]{2,1,0:T(8,128)(2,1)S(1)} all-to-all(bf16[16,40,256]{2,1,0:T(8,128)(2,1)S(1)} %get-tuple-element.50), channel_id=1, replica_groups=mesh['frames'=16,'tile'=8] {'frames'}, dimensions={0} | all-to-all | bytes 655360 | tf_op jit(solution)/shard_map/all_to_all | solution.py:492
  32.0 2.3 %collective-permute-start.4 = (bf16[16,40,256]{2,1,0:T(8,128)(2,1)S(1)}, bf16[16,40,256]{2,1,0:T(8,128)(2,1)S(1)}, u32[]{:S(2)}, u32[]{:S(2)}) collective-permute-start(bf16[16,40,256]{2,1,0:T(8,128)(2,1)S(1)} %all_to_all.5.refs_2_), channel_id=1, source_target_pairs={{0,1},{1,0},{2,3},{3,2},{4,5},{5,4},{6,7},{7,6},{8,9},{9,8},{10,11... | collective-permute-start | bytes 983048 | tf_op jit(solution)/shard_map/ppermute | solution.py:459
  34.3 2.2 %collective-permute-start.3 = (bf16[16,40,256]{2,1,0:T(8,128)(2,1)S(1)}, bf16[16,40,256]{2,1,0:T(8,128)(2,1)S(1)}, u32[]{:S(2)}, u32[]{:S(2)}) collective-permute-start(bf16[16,40,256]{2,1,0:T(8,128)(2,1)S(1)} %all_to_all.5.refs_2_), channel_id=1, source_target_pairs={{0,6},{1,7},{2,4},{3,5},{4,2},{5,3},{6,0},{7,1},{8,14},{9,15},{10,... | collective-permute-start | bytes 983048 | tf_op jit(solution)/shard_map/ppermute | solution.py:468
  36.5 0.8 %collective-permute-start.2 = (bf16[16,40,256]{2,1,0:T(8,128)(2,1)S(1)}, bf16[16,40,256]{2,1,0:T(8,128)(2,1)S(1)}, u32[]{:S(2)}, u32[]{:S(2)}) collective-permute-start(bf16[16,40,256]{2,1,0:T(8,128)(2,1)S(1)} %all_to_all.5.refs_2_), channel_id=1, source_target_pairs={{0,2},{1,3},{2,0},{3,1},{4,6},{5,7},{6,4},{7,5},{8,10},{9,11},{10,... | collective-permute-start | bytes 983048 | tf_op jit(solution)/shard_map/ppermute | solution.py:468
  37.3 1.1 %turn_queries.1 = (bf16[1280,256]{1,0:T(8,128)(2,1)S(1)}, bf16[1280,256]{1,0:T(8,128)(2,1)S(1)}, f32[8,640]{1,0:T(8,128)S(1)}) custom-call(bf16[64,2560]{1,0:T(8,128)(2,1)S(1)} %copy-done.1, bf16[256,2560]{1,0:T(8,128)(2,1)S(1)} %copy-done, s32[16,128]{1,0:T(8,128)S(1)} %get-tuple-element.45.frames_ref, s32[16,128]{1,0:T(8,128)S(1)} %get-tuple-element.46.blocks_ref), custom_call_target="tpu_custom_call" | custom-call | flops 83886080 | bytes 3145728 | tf_op jit(solution)/shard_map/turn_queries/pallas_call | solution.py:322
  38.4 3.4 %attend.4 = (f32[1280,128]{1,0:T(8,128)S(1)}, f32[1280,128]{1,0:T(8,128)S(1)}, f32[1280,256]{1,0:T(8,128)S(1)}) custom-call(bf16[1280,256]{1,0:T(8,128)(2,1)S(1)} %get-tuple-element.48.refs_0_, bf16[1280,256]{1,0:T(8,128)(2,1)S(1)} %get-tuple-element.49.refs_1_, bf16[16,40,256]{2,1,0:T(8,128)(2,1)S(1)} %all_to_all.5.refs_2_, ...), custom_call_target="tpu_custom_call" | custom-call | flops 2516582400 | bytes 6291456 | tf_op jit(solution)/shard_map/attend/pallas_call | solution.py:439
  41.8 2.9 %collective-permute-done.3.refs_3_ = bf16[16,40,256]{2,1,0:T(8,128)(2,1)S(1)} collective-permute-done((bf16[16,40,256]{2,1,0:T(8,128)(2,1)S(1)}, bf16[16,40,256]{2,1,0:T(8,128)(2,1)S(1)}, u32[]{:S(2)}, u32[]{:S(2)}) %collective-permute-start.3) | collective-permute-done | bytes 327712 | tf_op jit(solution)/shard_map/ppermute | solution.py:468
  44.7 0.7 %collective-permute-done.2.refs_2_ = bf16[16,40,256]{2,1,0:T(8,128)(2,1)S(1)} collective-permute-done((bf16[16,40,256]{2,1,0:T(8,128)(2,1)S(1)}, bf16[16,40,256]{2,1,0:T(8,128)(2,1)S(1)}, u32[]{:S(2)}, u32[]{:S(2)}) %collective-permute-start.2) | collective-permute-done | bytes 327712 | tf_op jit(solution)/shard_map/ppermute | solution.py:468
  45.5 1.1 %collective-permute-start.6 = (bf16[16,40,256]{2,1,0:T(8,128)(2,1)S(1)}, bf16[16,40,256]{2,1,0:T(8,128)(2,1)S(1)}, u32[]{:S(2)}, u32[]{:S(2)}) collective-permute-start(bf16[16,40,256]{2,1,0:T(8,128)(2,1)S(1)} %collective-permute-done.2.refs_2_), channel_id=1, source_target_pairs={{0,1},{1,0},{2,3},{3,2},{4,5},{5,4},{6,7},{7,6},{8,9},{9,8},{10,11... | collective-permute-start | bytes 983048 | tf_op jit(solution)/shard_map/ppermute | solution.py:459
  46.6 0.0 collective-permute-start.7
  46.7 0.8 %collective-permute-start.5 = (bf16[16,40,256]{2,1,0:T(8,128)(2,1)S(1)}, bf16[16,40,256]{2,1,0:T(8,128)(2,1)S(1)}, u32[]{:S(2)}, u32[]{:S(2)}) collective-permute-start(bf16[16,40,256]{2,1,0:T(8,128)(2,1)S(1)} %broadcast_select_fusion), channel_id=1, source_target_pairs={{0,6},{1,3},{2,4},{3,1},{4,2},{5,7},{6,0},{7,5},{8,14},{9,11},{10,... | collective-permute-start | bytes 983048 | tf_op jit(solution)/shard_map/ppermute | solution.py:468
  47.5 3.7 %attend.5 = (f32[1280,128]{1,0:T(8,128)S(1)}, f32[1280,128]{1,0:T(8,128)S(1)}, f32[1280,256]{1,0:T(8,128)S(1)}) custom-call(bf16[1280,256]{1,0:T(8,128)(2,1)S(1)} %get-tuple-element.48.refs_0_, bf16[1280,256]{1,0:T(8,128)(2,1)S(1)} %get-tuple-element.49.refs_1_, bf16[16,40,256]{2,1,0:T(8,128)(2,1)S(1)} %collective-permute-done.2.refs_2_, ...), custom_call_target="tpu_custom_call" | custom-call | flops 2516582400 | bytes 6291456 | tf_op jit(solution)/shard_map/attend/pallas_call | solution.py:439
  51.2 0.0 copy-start.2
  51.2 3.8 %attend.6 = (f32[1280,128]{1,0:T(8,128)S(1)}, f32[1280,128]{1,0:T(8,128)S(1)}, f32[1280,256]{1,0:T(8,128)S(1)}) custom-call(bf16[1280,256]{1,0:T(8,128)(2,1)S(1)} %get-tuple-element.48.refs_0_, bf16[1280,256]{1,0:T(8,128)(2,1)S(1)} %get-tuple-element.49.refs_1_, bf16[16,40,256]{2,1,0:T(8,128)(2,1)S(1)} %collective-permute-done.6.refs_2_, ...), custom_call_target="tpu_custom_call" | custom-call | flops 2516582400 | bytes 6291456 | tf_op jit(solution)/shard_map/attend/pallas_call | solution.py:439
  55.1 1.5 %collective-permute-start.8 = (bf16[16,40,256]{2,1,0:T(8,128)(2,1)S(1)}, bf16[16,40,256]{2,1,0:T(8,128)(2,1)S(1)}, u32[]{:S(2)}, u32[]{:S(2)}) collective-permute-start(bf16[16,40,256]{2,1,0:T(8,128)(2,1)S(1)} %collective-permute-done.5.refs_2_), channel_id=1, source_target_pairs={{0,1},{1,0},{2,3},{3,2},{4,5},{5,4},{6,7},{7,6},{8,9},{9,8},{10,11... | collective-permute-start | bytes 983048 | tf_op jit(solution)/shard_map/ppermute | solution.py:459
  56.6 1.3 %collective-permute-done.8.refs_3_ = bf16[16,40,256]{2,1,0:T(8,128)(2,1)S(1)} collective-permute-done((bf16[16,40,256]{2,1,0:T(8,128)(2,1)S(1)}, bf16[16,40,256]{2,1,0:T(8,128)(2,1)S(1)}, u32[]{:S(2)}, u32[]{:S(2)}) %collective-permute-start.8) | collective-permute-done | bytes 327712 | tf_op jit(solution)/shard_map/ppermute | solution.py:459
  57.9 5.3 %attend.7 = bf16[64,2560]{1,0:T(8,128)(2,1)} custom-call(bf16[1280,256]{1,0:T(8,128)(2,1)S(1)} %get-tuple-element.48.refs_0_, bf16[1280,256]{1,0:T(8,128)(2,1)S(1)} %get-tuple-element.49.refs_1_, bf16[16,40,256]{2,1,0:T(8,128)(2,1)S(1)} %collective-permute-done.5.refs_2_, bf16[16,40,256]{2,1,0:T(8,128)(2,1)S(1)} %collective-permute-done.8.refs_3_, ...), custom_call_target="tpu_custom_call" | custom-call | flops 2516582400 | bytes 6291456 | tf_op jit(solution)/shard_map/attend/pallas_call | solution.py:439
  (10 shorter events, 0.1 us)
Async XLA Ops:
  1.7 10.9 %collective-permute-start.1 = (bf16[2,160,256]{2,1,0:T(8,128)(2,1)S(1)}, bf16[2,160,256]{2,1,0:T(8,128)(2,1)S(1)}, u32[]{:S(2)}, u32[]{:S(2)}) collective-permute-start(bf16[2,160,256]{2,1,0:T(8,128)(2,1)S(1)} %get-tuple-element.70), channel_id=1, source_target_pairs={{1,2},{2,1},{3,4},{4,3},{5,6},{6,5},{9,10},{10,9},{11,12},{12,11},... | collective-permute-start | bytes 491528 | tf_op jit(solution)/shard_map/ppermute | solution.py:481
  6.6 6.0 %collective-permute-start = (bf16[2,160,256]{2,1,0:T(8,128)(2,1)S(1)}, bf16[2,160,256]{2,1,0:T(8,128)(2,1)S(1)}, u32[]{:S(2)}, u32[]{:S(2)}) collective-permute-start(bf16[2,160,256]{2,1,0:T(8,128)(2,1)S(1)} %get-tuple-element.71), channel_id=1, source_target_pairs={{0,1},{1,0},{2,3},{3,2},{4,5},{5,4},{6,7},{7,6},{8,9},{9,8},{10,11... | collective-permute-start | bytes 491528 | tf_op jit(solution)/shard_map/ppermute | solution.py:459
  12.6 24.7 %copy-start = (bf16[256,2560]{1,0:T(8,128)(2,1)S(1)}, bf16[256,2560]{1,0:T(8,128)(2,1)}, u32[]{:S(2)}) copy-start(bf16[256,2560]{1,0:T(8,128)(2,1)} %wk_ref.1) | copy-start | bytes 3932164
  12.6 24.7 %copy-start.1 = (bf16[64,2560]{1,0:T(8,128)(2,1)S(1)}, bf16[64,2560]{1,0:T(8,128)(2,1)}, u32[]{:S(2)}) copy-start(bf16[64,2560]{1,0:T(8,128)(2,1)} %q_ref.1) | copy-start | bytes 983044
  32.0 6.4 %collective-permute-start.4 = (bf16[16,40,256]{2,1,0:T(8,128)(2,1)S(1)}, bf16[16,40,256]{2,1,0:T(8,128)(2,1)S(1)}, u32[]{:S(2)}, u32[]{:S(2)}) collective-permute-start(bf16[16,40,256]{2,1,0:T(8,128)(2,1)S(1)} %all_to_all.5.refs_2_), channel_id=1, source_target_pairs={{0,1},{1,0},{2,3},{3,2},{4,5},{5,4},{6,7},{7,6},{8,9},{9,8},{10,11... | collective-permute-start | bytes 983048 | tf_op jit(solution)/shard_map/ppermute | solution.py:459
  34.3 10.5 %collective-permute-start.3 = (bf16[16,40,256]{2,1,0:T(8,128)(2,1)S(1)}, bf16[16,40,256]{2,1,0:T(8,128)(2,1)S(1)}, u32[]{:S(2)}, u32[]{:S(2)}) collective-permute-start(bf16[16,40,256]{2,1,0:T(8,128)(2,1)S(1)} %all_to_all.5.refs_2_), channel_id=1, source_target_pairs={{0,6},{1,7},{2,4},{3,5},{4,2},{5,3},{6,0},{7,1},{8,14},{9,15},{10,... | collective-permute-start | bytes 983048 | tf_op jit(solution)/shard_map/ppermute | solution.py:468
  36.5 9.0 %collective-permute-start.2 = (bf16[16,40,256]{2,1,0:T(8,128)(2,1)S(1)}, bf16[16,40,256]{2,1,0:T(8,128)(2,1)S(1)}, u32[]{:S(2)}, u32[]{:S(2)}) collective-permute-start(bf16[16,40,256]{2,1,0:T(8,128)(2,1)S(1)} %all_to_all.5.refs_2_), channel_id=1, source_target_pairs={{0,2},{1,3},{2,0},{3,1},{4,6},{5,7},{6,4},{7,5},{8,10},{9,11},{10,... | collective-permute-start | bytes 983048 | tf_op jit(solution)/shard_map/ppermute | solution.py:468
  45.5 5.7 %collective-permute-start.6 = (bf16[16,40,256]{2,1,0:T(8,128)(2,1)S(1)}, bf16[16,40,256]{2,1,0:T(8,128)(2,1)S(1)}, u32[]{:S(2)}, u32[]{:S(2)}) collective-permute-start(bf16[16,40,256]{2,1,0:T(8,128)(2,1)S(1)} %collective-permute-done.2.refs_2_), channel_id=1, source_target_pairs={{0,1},{1,0},{2,3},{3,2},{4,5},{5,4},{6,7},{7,6},{8,9},{9,8},{10,11... | collective-permute-start | bytes 983048 | tf_op jit(solution)/shard_map/ppermute | solution.py:459
  46.6 4.6 %collective-permute-start.7 = (bf16[16,40,256]{2,1,0:T(8,128)(2,1)S(1)}, bf16[16,40,256]{2,1,0:T(8,128)(2,1)S(1)}, u32[]{:S(2)}, u32[]{:S(2)}) collective-permute-start(bf16[16,40,256]{2,1,0:T(8,128)(2,1)S(1)} %collective-permute-done.3.refs_3_), channel_id=1, source_target_pairs={{0,1},{1,0},{2,3},{3,2},{4,5},{5,4},{6,7},{7,6},{8,9},{9,8},{10,11... | collective-permute-start | bytes 983048 | tf_op jit(solution)/shard_map/ppermute | solution.py:459
  46.7 8.4 %collective-permute-start.5 = (bf16[16,40,256]{2,1,0:T(8,128)(2,1)S(1)}, bf16[16,40,256]{2,1,0:T(8,128)(2,1)S(1)}, u32[]{:S(2)}, u32[]{:S(2)}) collective-permute-start(bf16[16,40,256]{2,1,0:T(8,128)(2,1)S(1)} %broadcast_select_fusion), channel_id=1, source_target_pairs={{0,6},{1,3},{2,4},{3,1},{4,2},{5,7},{6,0},{7,5},{8,14},{9,11},{10,... | collective-permute-start | bytes 983048 | tf_op jit(solution)/shard_map/ppermute | solution.py:468
  51.2 6.7 %copy-start.2 = (bf16[256,2560]{1,0:T(8,128)(2,1)S(1)}, bf16[256,2560]{1,0:T(8,128)(2,1)}, u32[]{:S(2)}) copy-start(bf16[256,2560]{1,0:T(8,128)(2,1)} %refs_8_.1) | copy-start | bytes 3932164
  55.1 2.8 %collective-permute-start.8 = (bf16[16,40,256]{2,1,0:T(8,128)(2,1)S(1)}, bf16[16,40,256]{2,1,0:T(8,128)(2,1)S(1)}, u32[]{:S(2)}, u32[]{:S(2)}) collective-permute-start(bf16[16,40,256]{2,1,0:T(8,128)(2,1)S(1)} %collective-permute-done.5.refs_2_), channel_id=1, source_target_pairs={{0,1},{1,0},{2,3},{3,2},{4,5},{5,4},{6,7},{7,6},{8,9},{9,8},{10,11... | collective-permute-start | bytes 983048 | tf_op jit(solution)/shard_map/ppermute | solution.py:459
